TPU v7x, 8 devices: a whole 2x2x1 slice. The times are simulated.
8 devices in a mesh: dp: 2 (over z, y), tp: 4 (over x, core).
Axes of the slice: x: 2, y: 2, z: 1, core: 2. Of those that a mesh axis runs over, the one named last changes fastest.
Arguments:
- hidden: bfloat16 [48, 2560], P('dp'), parts along dimension 0
- positions: int32 [48], P('dp'), parts along dimension 0
- k_local: bfloat16 [48, 1024, 4, 256], P('dp', None, 'tp'), parts along dimension 0
- v_local: bfloat16 [48, 1024, 4, 256], P('dp', None, 'tp'), parts along dimension 0
- k_global: bfloat16 [48, 2048, 4, 256], P('dp', None, 'tp'), parts along dimension 0
- v_global: bfloat16 [48, 2048, 4, 256], P('dp', None, 'tp'), parts along dimension 0
- w_query: bfloat16 [2, 2560, 2048], P(None, None, 'tp')
- w_key: bfloat16 [2, 2560, 1024], P(None, None, 'tp')
- w_value: bfloat16 [2, 2560, 1024], P(None, None, 'tp')
- w_out: bfloat16 [2, 2048, 2560], P(None, 'tp')
- w_gate: bfloat16 [2, 2560, 10240], P(None, None, 'tp')
- w_up: bfloat16 [2, 2560, 10240], P(None, None, 'tp')
- w_down: bfloat16 [2, 10240, 2560], P(None, 'tp')
- norm_scale: float32 [2, 4, 2560], replicated
Outputs:
- output 1: bfloat16 [48, 2560], P('dp'), parts along dimension 0
- output 2: bfloat16 [48, 1024, 4, 256], P('dp', None, 'tp'), parts along dimension 0
- output 3: bfloat16 [48, 1024, 4, 256], P('dp', None, 'tp'), parts along dimension 0
- output 4: bfloat16 [48, 2048, 4, 256], P('dp', None, 'tp'), parts along dimension 0
- output 5: bfloat16 [48, 2048, 4, 256], P('dp', None, 'tp'), parts along dimension 0
There are 2 independent parts. A program takes and returns all parts, laid end to end along the dimension named above; an argument that names none is the same for every part.
All inputs are finite; a program needn't handle non-finite values.
Results may differ from a plain program's by a relative error of at most 0.02.
Values are sent between devices in bfloat16 or wider.
A program may use at most 1 GiB of HBM per device.

v0:
```python
import jax
import jax.numpy as jnp
from jax import lax
from jax.sharding import PartitionSpec as P

SOFT_CAP = 50.0
NORM_EPS = 1e-6
ROPE_BASE = 10000.0
NEG_FILL = -1e30


def rms_norm(values, gain_row):
    values_f32 = values.astype(jnp.float32)
    inv_rms = lax.rsqrt(jnp.mean(values_f32 * values_f32, axis=-1, keepdims=True) + NORM_EPS)
    return (values_f32 * inv_rms * (1.0 + gain_row)).astype(jnp.bfloat16)


def rotary(projected, positions):
    head_dim = projected.shape[-1]
    half_dim = head_dim // 2
    inv_freq = ROPE_BASE ** (-2.0 * jnp.arange(half_dim, dtype=jnp.float32) / head_dim)
    angles = positions.astype(jnp.float32)[:, None, None] * inv_freq
    cos_part = jnp.cos(angles)
    sin_part = jnp.sin(angles)
    first_half = projected[..., :half_dim]
    second_half = projected[..., half_dim:]
    return jnp.concatenate([first_half * cos_part - second_half * sin_part, second_half * cos_part + first_half * sin_part], axis=-1)


def project_and_store(hidden, positions, k_cache, v_cache, slot_ids, w_query, w_key, w_value, gain_row):
    batch_rows = hidden.shape[0]
    kv_count = k_cache.shape[2]
    head_dim = k_cache.shape[3]
    normed = rms_norm(hidden, gain_row)
    queries = rotary(jnp.dot(normed, w_query, preferred_element_type=jnp.float32).reshape(batch_rows, -1, head_dim), positions)
    key_new = rotary(jnp.dot(normed, w_key, preferred_element_type=jnp.float32).reshape(batch_rows, kv_count, head_dim), positions)
    value_new = jnp.dot(normed, w_value, preferred_element_type=jnp.float32).reshape(batch_rows, kv_count, head_dim)
    slot_iota = lax.broadcasted_iota(jnp.int32, (batch_rows, k_cache.shape[1]), 1)
    slot_hit = (slot_iota == slot_ids[:, None])[:, :, None, None]
    k_cache = jnp.where(slot_hit, key_new.astype(jnp.bfloat16)[:, None], k_cache)
    v_cache = jnp.where(slot_hit, value_new.astype(jnp.bfloat16)[:, None], v_cache)
    grouped = queries.astype(jnp.bfloat16).reshape(batch_rows, kv_count, -1, head_dim)
    return grouped, k_cache, v_cache


def attention(grouped, k_cache, v_cache, key_valid):
    head_dim = grouped.shape[-1]
    logits = jnp.einsum('bgrd,bngd->bgrn', grouped, k_cache, preferred_element_type=jnp.float32) * head_dim ** -0.5
    logits = SOFT_CAP * jnp.tanh(logits / SOFT_CAP)
    if key_valid is not None:
        logits = jnp.where(key_valid[:, None, None, :], logits, NEG_FILL)
    attn_probs = jax.nn.softmax(logits, axis=-1).astype(jnp.bfloat16)
    mixed_heads = jnp.einsum('bgrn,bngd->bgrd', attn_probs, v_cache, preferred_element_type=jnp.float32)
    return mixed_heads.astype(jnp.bfloat16)


def mlp_part(normed, w_gate, w_up, w_down):
    gate_proj = jnp.dot(normed, w_gate, preferred_element_type=jnp.float32)
    up_proj = jnp.dot(normed, w_up, preferred_element_type=jnp.float32)
    hidden_act = (jax.nn.gelu(gate_proj, approximate=True) * up_proj).astype(jnp.bfloat16)
    return jnp.dot(hidden_act, w_down, preferred_element_type=jnp.float32)


def add_normed(hidden, branch_sum, gain_row):
    return (hidden.astype(jnp.float32) + rms_norm(branch_sum, gain_row).astype(jnp.float32)).astype(jnp.bfloat16)


def decoder_layer(hidden, positions, k_cache, v_cache, slot_ids, key_valid, layer_weights, gains):
    w_query, w_key, w_value, w_out, w_gate, w_up, w_down = layer_weights
    grouped, k_cache, v_cache = project_and_store(hidden, positions, k_cache, v_cache, slot_ids, w_query, w_key, w_value, gains[0])
    mixed_heads = attention(grouped, k_cache, v_cache, key_valid)
    attn_part = jnp.dot(mixed_heads.reshape(hidden.shape[0], -1), w_out, preferred_element_type=jnp.float32)
    attn_sum = lax.psum(attn_part.astype(jnp.bfloat16), 'tp')
    hidden = add_normed(hidden, attn_sum, gains[1])
    down_part = mlp_part(rms_norm(hidden, gains[2]), w_gate, w_up, w_down)
    down_sum = lax.psum(down_part.astype(jnp.bfloat16), 'tp')
    hidden = add_normed(hidden, down_sum, gains[3])
    return hidden, k_cache, v_cache


def decode_step(hidden, positions, k_local, v_local, k_global, v_global, w_query, w_key, w_value, w_out, w_gate, w_up, w_down, norm_scale):
    stacks = (w_query, w_key, w_value, w_out, w_gate, w_up, w_down)
    window = k_local.shape[1]
    global_valid = lax.broadcasted_iota(jnp.int32, (hidden.shape[0], k_global.shape[1]), 1) <= positions[:, None]
    hidden, k_local, v_local = decoder_layer(hidden, positions, k_local, v_local, positions % window, None, tuple(stacked[0] for stacked in stacks), norm_scale[0])
    hidden, k_global, v_global = decoder_layer(hidden, positions, k_global, v_global, positions, global_valid, tuple(stacked[1] for stacked in stacks), norm_scale[1])
    return hidden, k_local, v_local, k_global, v_global


def solution(mesh):
    row_spec = P('dp', None)
    cache_spec = P('dp', None, 'tp', None)
    col_split = P(None, None, 'tp')
    row_split = P(None, 'tp', None)
    in_specs = (row_spec, P('dp'), cache_spec, cache_spec, cache_spec, cache_spec, col_split, col_split, col_split, row_split, col_split, col_split, row_split, P())
    out_specs = (row_spec, cache_spec, cache_spec, cache_spec, cache_spec)
    return jax.shard_map(decode_step, mesh=mesh, in_specs=in_specs, out_specs=out_specs, check_vma=False)
```

profile of v0, /device:TPU:0, one launch (start us, length us, event | category | flops | bytes accessed | tf_op | source)
XLA Modules:
  0.0 281.5 jit_solution(10174441267240137521)
XLA Ops:
  10.5 1.7 fusion.90
  12.2 1.7 fusion.84
  14.2 4.4 %slice_bitcast_fusion = (bf16[512,2560]{0,1:T(8,128)(2,1)S(1)}, bf16[512,2560]{0,1:T(8,128)(2,1)}) fusion(bf16[2,2560,512]{2,1,0:T(8,128)(2,1)} %param.20), kind=kLoop, calls=%fused_computation.43 | loop fusion | bytes 10485760 | tf_op jit(solution)/shard_map/dot_general | solution.py:35
  18.5 4.4 %copy.19 = bf16[512,2560]{1,0:T(8,128)(2,1)} copy(bf16[512,2560]{0,1:T(8,128)(2,1)} %get-tuple-element.20) | data formatting | bytes 5242880 | tf_op jit(solution)/shard_map/dot_general | solution.py:35
  22.9 2.5 fusion.158
  25.5 13.6 %broadcast_select_fusion.3 = (bf16[24,1024,1,256]{3,1,2,0:T(8,128)(2,1)S(1)}, bf16[24,1024,1,256]{3,1,2,0:T(8,128)(2,1)}) fusion(bf16[24,1024,1,256]{3,1,2,0:T(8,128)(2,1)} %param.16, pred[24,1024]{1,0:T(8,128)(4,1)S(1)} %iota_compare_fusion.2, bf16[24,256]{1,0:T(8,128)(2,1)S(1)} %pad_maximum_fusion.2, bf16[24,1024,1,256]{3,1,2,0:T(8,128)(2,1)} %param.17, ...), kind=kLoop, calls=%fused_computation.31 | loop fusion | flops 12582912 | bytes 50380800 | tf_op jit(solution)/shard_map/jit(_where)/select_n | solution.py:40
  39.1 4.8 %copy-done = bf16[24,1024,1,256]{3,1,2,0:T(8,128)(2,1)} copy-done((bf16[24,1024,1,256]{3,1,2,0:T(8,128)(2,1)}, bf16[24,1024,1,256]{3,1,2,0:T(8,128)(2,1)S(1)}, u32[]{:S(2)}) %copy-start) | copy-done | bytes 12582936
  43.9 3.3 %fusion.102 = f32[24,2,1024]{2,1,0:T(2,128)S(1)} fusion(bf16[24,1024,1,256]{3,1,2,0:T(8,128)(2,1)S(1)} %get-tuple-element.31, bf16[24,2,256]{2,0,1:T(8,128)(2,1)S(1)} %pad_maximum_fusion), kind=kOutput, calls=%fused_computation.74 | convolution fusion | flops 25264128 | bytes 12804096 | tf_op jit(solution)/shard_map/bgrd,bngd->bgrn/dot_general | solution.py:48
  47.5 6.4 %fusion.78 = bf16[24,2,256]{2,1,0:T(2,128)(2,1)S(1)} fusion(bf16[24,1024,1,256]{3,1,2,0:T(8,128)(2,1)} %get-tuple-element.32, f32[24,2]{1,0:T(8,128)S(1)} %fusion.200, f32[24,2,1024]{2,1,0:T(2,128)S(1)} %fusion.102), kind=kOutput, calls=%fused_computation.66 | convolution fusion | flops 25326640 | bytes 12804288 | tf_op jit(solution)/shard_map/bgrn,bngd->bgrd/dot_general | solution.py:53
  53.9 2.9 %convolution_convert_fusion.1 = bf16[24,2560]{1,0:T(8,128)(2,1)} fusion(bf16[24,512]{1,0:T(8,128)(2,1)S(1)} %bitcast.137, bf16[2,512,2560]{2,1,0:T(8,128)(2,1)} %param.23), kind=kOutput, calls=%fused_computation.35 | convolution fusion | flops 62976000 | bytes 2768896 | tf_op jit(solution)/shard_map/dot_general | solution.py:72
  56.9 28.9 %all-reduce.5.cloned.1.call-done = bf16[24,2560]{1,0:T(8,128)(2,1)} async-done(((bf16[24,2560]{1,0:T(8,128)(2,1)}), bf16[24,2560]{1,0:T(8,128)(2,1)}) %all-reduce.5.cloned.1.call-update) | async-done | bytes 122896 | tf_op jit(solution)/shard_map/psum | solution.py:73
  88.0 5.8 %fusion.135 = f32[24,2560]{1,0:T(8,128)S(1)} fusion(bf16[2,2560,2560]{2,1,0:T(8,128)(2,1)} %param.24, bf16[24,2560]{1,0:T(8,128)(2,1)S(1)} %get-tuple-element.18, f32[2560]{0:T(1024)S(1)} %get-tuple-element.9, f32[24]{0:T(128)S(1)} %add_rsqrt_fusion.5), kind=kOutput, calls=%fused_computation.124 | convolution fusion | flops 315310080 | bytes 13486176 | tf_op jit(solution)/shard_map/dot_general | solution.py:58
  93.8 11.3 %fusion.40 = bf16[24,2560]{1,0:T(8,128)(2,1)} fusion(bf16[2,2560,2560]{2,1,0:T(8,128)(2,1)} %param.26, f32[24,2560]{1,0:T(8,128)S(1)} %fusion.135, bf16[2,2560,2560]{2,1,0:T(8,128)(2,1)} %param.25, bf16[24,2560]{1,0:T(8,128)(2,1)S(1)} %get-tuple-element.18, f32[2560]{0:T(1024)S(1)} %get-tuple-element.9, f32[24]{0:T(128)S(1)} %add_rsqrt_fusion.5), kind=kOutput, calls=%fused_computation.38 | convolution fusion | flops 629575680 | bytes 26716256 | tf_op jit(solution)/shard_map/dot_general | solution.py:61
  105.5 2.8 copy.21
  108.3 23.1 %all-reduce.7.cloned.1.call-done = bf16[24,2560]{1,0:T(8,128)(2,1)} async-done(((bf16[24,2560]{1,0:T(8,128)(2,1)}), bf16[24,2560]{1,0:T(8,128)(2,1)}) %all-reduce.7.cloned.1.call-update) | async-done | bytes 122896 | tf_op jit(solution)/shard_map/psum | solution.py:76
  136.9 2.5 fusion.156
  139.6 34.3 %broadcast_select_fusion.1 = (bf16[24,2048,1,256]{3,1,2,0:T(8,128)(2,1)}, bf16[24,2048,1,256]{3,1,2,0:T(8,128)(2,1)}) fusion(bf16[24,2048,1,256]{3,1,2,0:T(8,128)(2,1)} %param.18, pred[24,2048]{1,0:T(8,128)(4,1)S(1)} %get-tuple-element.36, bf16[24,256]{1,0:T(8,128)(2,1)S(1)} %pad_maximum_fusion.3, bf16[24,2048,1,256]{3,1,2,0:T(8,128)(2,1)} %param.19, ...), kind=kLoop, calls=%fused_computation.7 | loop fusion | flops 25165824 | bytes 100737024 | tf_op jit(solution)/shard_map/jit(_where)/select_n | solution.py:40
  173.9 11.5 %fusion.61 = f32[24,2,2048]{2,1,0:T(2,128)S(1)} fusion(bf16[24,2048,1,256]{3,1,2,0:T(8,128)(2,1)} %get-tuple-element.25, pred[24,2048]{1,0:T(8,128)(4,1)S(1)} %get-tuple-element.35, bf16[24,2,256]{2,0,1:T(8,128)(2,1)S(1)} %pad_maximum_fusion.1), kind=kOutput, calls=%fused_computation.51 | convolution fusion | flops 50626560 | bytes 25632768 | tf_op jit(solution)/shard_map/bgrd,bngd->bgrn/dot_general | solution.py:48
  185.9 11.6 %fusion.81 = bf16[24,2,256]{2,1,0:T(2,128)(2,1)S(1)} fusion(bf16[24,2048,1,256]{3,1,2,0:T(8,128)(2,1)} %get-tuple-element.26, f32[24,2]{1,0:T(8,128)S(1)} %fusion.201, f32[24,2,2048]{2,1,0:T(2,128)S(1)} %fusion.61), kind=kOutput, calls=%fused_computation.67 | convolution fusion | flops 50640944 | bytes 25583808 | tf_op jit(solution)/shard_map/bgrn,bngd->bgrd/dot_general | solution.py:53
  197.5 2.9 %convolution_convert_fusion = bf16[24,2560]{1,0:T(8,128)(2,1)} fusion(bf16[24,512]{1,0:T(8,128)(2,1)S(1)} %bitcast.138, bf16[2,512,2560]{2,1,0:T(8,128)(2,1)} %param.23), kind=kOutput, calls=%fused_computation.34 | convolution fusion | flops 62976000 | bytes 2768896 | tf_op jit(solution)/shard_map/dot_general | solution.py:72
  200.4 26.2 %all-reduce.9.cloned.1.call-done = bf16[24,2560]{1,0:T(8,128)(2,1)} async-done(((bf16[24,2560]{1,0:T(8,128)(2,1)}), bf16[24,2560]{1,0:T(8,128)(2,1)}) %all-reduce.9.cloned.1.call-update) | async-done | bytes 122896 | tf_op jit(solution)/shard_map/psum | solution.py:73
  228.8 5.8 %fusion.152 = f32[24,2560]{1,0:T(8,128)S(1)} fusion(bf16[2,2560,2560]{2,1,0:T(8,128)(2,1)} %param.24, bf16[24,2560]{1,0:T(8,128)(2,1)S(1)} %get-tuple-element.14, f32[2560]{0:T(1024)S(1)} %get-tuple-element.12, f32[24]{0:T(128)S(1)} %add_rsqrt_fusion.1), kind=kOutput, calls=%fused_computation.139 | convolution fusion | flops 315310080 | bytes 13486176 | tf_op jit(solution)/shard_map/dot_general | solution.py:58
  234.7 11.3 %fusion.43 = bf16[24,2560]{1,0:T(8,128)(2,1)} fusion(bf16[2,2560,2560]{2,1,0:T(8,128)(2,1)} %param.26, f32[24,2560]{1,0:T(8,128)S(1)} %fusion.152, bf16[2,2560,2560]{2,1,0:T(8,128)(2,1)} %param.25, bf16[24,2560]{1,0:T(8,128)(2,1)S(1)} %get-tuple-element.14, f32[2560]{0:T(1024)S(1)} %get-tuple-element.12, f32[24]{0:T(128)S(1)} %add_rsqrt_fusion.1), kind=kOutput, calls=%fused_computation.39 | convolution fusion | flops 629575680 | bytes 26716256 | tf_op jit(solution)/shard_map/dot_general | solution.py:61
  246.0 26.2 %all-reduce.11.cloned.1.call-done = bf16[24,2560]{1,0:T(8,128)(2,1)} async-done(((bf16[24,2560]{1,0:T(8,128)(2,1)}), bf16[24,2560]{1,0:T(8,128)(2,1)}) %all-reduce.11.cloned.1.call-update) | async-done | bytes 122896 | tf_op jit(solution)/shard_map/psum | solution.py:76
  (50 shorter events, 17.6 us)
Async XLA Ops:
  7.2 15.8 %copy-start.1 = (bf16[24,2560]{1,0:T(8,128)(2,1)S(1)}, bf16[24,2560]{1,0:T(8,128)(2,1)}, u32[]{:S(2)}) copy-start(bf16[24,2560]{1,0:T(8,128)(2,1)} %param.14) | copy-start | bytes 368644
  7.2 78.6 %all-reduce.5.cloned.1.call-start = ((), (), s32[]{:S(2)}) async-start(), calls=%async_computation | async-start | bytes 245760 | tf_op jit(solution)/shard_map/psum | solution.py:73
  39.1 4.8 %copy-start = (bf16[24,1024,1,256]{3,1,2,0:T(8,128)(2,1)}, bf16[24,1024,1,256]{3,1,2,0:T(8,128)(2,1)S(1)}, u32[]{:S(2)}) copy-start(bf16[24,1024,1,256]{3,1,2,0:T(8,128)(2,1)S(1)} %get-tuple-element.31) | copy-start | bytes 37748740
  56.8 74.6 %all-reduce.7.cloned.1.call-start = ((), (), s32[]{:S(2)}) async-start(), calls=%async_computation.1 | async-start | bytes 245760 | tf_op jit(solution)/shard_map/psum | solution.py:76
  93.8 11.6 %copy-start.2 = (s32[24]{0:T(128)S(1)}, s32[24]{0:T(128)}, u32[]{:S(2)}) copy-start(s32[24]{0:T(128)} %param.15) | copy-start | bytes 292
  105.1 121.5 %all-reduce.9.cloned.1.call-start = ((), (), s32[]{:S(2)}) async-start(), calls=%async_computation.2 | async-start | bytes 245760 | tf_op jit(solution)/shard_map/psum | solution.py:73
  200.4 71.8 %all-reduce.11.cloned.1.call-start = ((), (), s32[]{:S(2)}) async-start(), calls=%async_computation.3 | async-start | bytes 245760 | tf_op jit(solution)/shard_map/psum | solution.py:76
Sparse Core Ops, SparseCore 0:
  56.9 28.7 all-reduce.4
  105.2 26.0 all-reduce.6
  200.5 26.0 all-reduce.8
  246.1 26.0 all-reduce.10
where the time goes:
time: 282 us; the launch traced here: 281 us
  waiting for transfers between devices  105 us (37%)
  matrix products  84.6 us (30%)
  other arithmetic  61.8 us (22%)
  local copies, waits for them, and re-layouts  16.3 us (6%)
  between operations  13.9 us (5%)
    psum x2, waiting for transfers between devices, decoder_layer(): attn_sum = lax.psum(attn_part.astype(jnp.bfloat16), 'tp')  55.1 us
    psum x2, waiting for transfers between devices, decoder_layer(): down_sum = lax.psum(down_part.astype(jnp.bfloat16), 'tp')  49.4 us
    select_n x2, other arithmetic, project_and_store(): jnp.where(slot_hit, key_new.astype(jnp.bfloat16)[:, None], k_cache)  47.9 us
    dot_general x2, matrix products, mlp_part(): return jnp.dot(hidden_act, w_down, preferred_element_type=jnp.float32)  22.6 us
    dot_general x2, matrix products, attention(): jnp.einsum('bgrn,bngd->bgrd', attn_probs, v_cache, preferred_element_type...  18 us
    dot_general x2, matrix products, attention(): jnp.einsum('bgrd,bngd->bgrn', grouped, k_cache, preferred_element_type=jn...  14.9 us
    dot_general x2, matrix products, mlp_part(): gate_proj = jnp.dot(normed, w_gate, preferred_element_type=jnp.float32)  11.6 us
    dot_general x3, local copies, waits for them, and re-layouts, project_and_store(): jnp.dot(normed, w_query, preferred_element_type=jnp.float32)  11.5 us
  transfers between devices with their start and end apart: 4, of which 4 were waited for; matrix products, arithmetic and copies ran while one was open for 1% of the time, Pallas kernels for 0%

commit v1 on v0

v1 whole, which is shorter than its diff:
```python
import functools

import jax
import jax.numpy as jnp
import numpy as np
from jax import lax
from jax.experimental import pallas as pl
from jax.experimental.pallas import tpu as pltpu
from jax.sharding import PartitionSpec as P

SOFT_CAP = 50.0
NORM_EPS = 1e-6
ROPE_BASE = 10000.0
ROWS = 24
D = 2560
HEAD = 256
HALF = 128
GROUP = 4
SLOTS = 4
CHUNK = 512
F32 = jnp.float32
BF16 = jnp.bfloat16


def normed(values, gain_row):
    inv_rms = lax.rsqrt(jnp.mean(values * values, axis=-1, keepdims=True) + NORM_EPS)
    return (values * inv_rms * (1.0 + gain_row)).astype(BF16)


def attn_kernel(layer, masked, pos_hbm, x_hbm, gain_hbm, freq_hbm, wq_hbm, wk_hbm, wv_hbm, wo_hbm, kc_hbm, vc_hbm,
                ko_hbm, vo_hbm, o_ref,
                pos, x, gain, freq, wq, wk, wv, wo, kbuf, vbuf, qa, qb, ma, mb, knew, vnew,
                small_sem, w_sem, kr_sem, vr_sem, kw_sem, vw_sem):
    n = kc_hbm.shape[1]
    groups = ROWS // GROUP

    def rows_of(ref, g):
        return ref.at[pl.ds(g * GROUP, GROUP)]

    def read(g, slot):
        pltpu.make_async_copy(rows_of(kc_hbm, g), kbuf.at[slot], kr_sem.at[slot]).start()
        pltpu.make_async_copy(rows_of(vc_hbm, g), vbuf.at[slot], vr_sem.at[slot]).start()

    small = [pltpu.make_async_copy(s, d, small_sem.at[i]) for i, (s, d) in enumerate(
        ((x_hbm, x), (gain_hbm.at[layer], gain), (pos_hbm, pos), (freq_hbm, freq)))]
    weights = [pltpu.make_async_copy(s.at[layer], d, w_sem.at[i]) for i, (s, d) in enumerate(
        ((wq_hbm, wq), (wk_hbm, wk), (wv_hbm, wv), (wo_hbm, wo)))]
    for copy in small:
        copy.start()
    for copy in weights[:3]:
        copy.start()
    for g in range(SLOTS):
        read(g, g)
    weights[3].start()

    for copy in small:
        copy.wait()
    a = normed(x[...].astype(F32), gain[0:1, :])
    row_ids = lax.broadcasted_iota(jnp.int32, (ROWS, HALF), 0)
    pos_rows = jnp.zeros((ROWS, HALF), jnp.int32)
    for b in range(ROWS):
        pos_rows = jnp.where(row_ids == b, pos[b], pos_rows)
    angles = pos_rows.astype(F32) * freq[...]
    cos_part = jnp.cos(angles)
    sin_part = jnp.sin(angles)

    def rotate(t):
        first, second = t[:, :HALF], t[:, HALF:]
        return first * cos_part - second * sin_part, second * cos_part + first * sin_part

    weights[0].wait()
    q = jnp.dot(a, wq[...], preferred_element_type=F32)
    for h in range(2):
        first, second = rotate(q[:, h * HEAD:(h + 1) * HEAD])
        qa[pl.ds(h, ROWS, stride=2), :] = first
        qb[pl.ds(h, ROWS, stride=2), :] = second
    weights[1].wait()
    first, second = rotate(jnp.dot(a, wk[...], preferred_element_type=F32))
    knew[:, :HALF] = first
    knew[:, HALF:] = second
    weights[2].wait()
    vnew[...] = jnp.dot(a, wv[...], preferred_element_type=F32)

    def patch(buf, slot, j, row, b, new):
        base = pl.multiple_of((row // 16) * 16, 16)
        tile = buf[slot, j, pl.ds(base, 16), :].astype(F32)
        hit = lax.broadcasted_iota(jnp.int32, (16, HEAD), 0) == row - base
        fresh = jnp.broadcast_to(new[pl.ds(b, 1), :], (16, HEAD))
        buf[slot, j, pl.ds(base, 16), :] = jnp.where(hit, fresh, tile).astype(BF16)

    def write_copies(g, slot):
        return (pltpu.make_async_copy(kbuf.at[slot], rows_of(ko_hbm, g), kw_sem.at[slot]),
                pltpu.make_async_copy(vbuf.at[slot], rows_of(vo_hbm, g), vw_sem.at[slot]))

    def step(g, carry):
        slot = lax.rem(g, SLOTS)
        pltpu.make_async_copy(rows_of(kc_hbm, g), kbuf.at[slot], kr_sem.at[slot]).wait()
        for j in range(GROUP):
            b = g * GROUP + j
            patch(kbuf, slot, j, lax.rem(pos[b], n), b, knew)
        q8 = jnp.concatenate([qa[pl.ds(pl.multiple_of(g * 8, 8), 8), :], qb[pl.ds(pl.multiple_of(g * 8, 8), 8), :]], axis=1).astype(BF16)
        owner = lax.broadcasted_iota(jnp.int32, (8, n), 0) // 2
        s = None
        for j in range(GROUP):
            part = lax.dot_general(q8, kbuf[slot, j], (((1,), (1,)), ((), ())), preferred_element_type=F32)
            s = part if s is None else jnp.where(owner == j, part, s)
        e = jnp.exp(SOFT_CAP * jnp.tanh(s * (HEAD ** -0.5 / SOFT_CAP)))
        if masked:
            limit_rows = lax.broadcasted_iota(jnp.int32, (8, 1), 0) // 2
            limit = jnp.zeros((8, 1), jnp.int32)
            for j in range(GROUP):
                limit = jnp.where(limit_rows == j, pos[g * GROUP + j], limit)
            e = jnp.where(lax.broadcasted_iota(jnp.int32, (8, n), 1) <= limit, e, 0.0)
        p = (e / jnp.sum(e, axis=-1, keepdims=True)).astype(BF16)
        pltpu.make_async_copy(rows_of(vc_hbm, g), vbuf.at[slot], vr_sem.at[slot]).wait()
        for j in range(GROUP):
            b = g * GROUP + j
            patch(vbuf, slot, j, lax.rem(pos[b], n), b, vnew)
        owner = lax.broadcasted_iota(jnp.int32, (8, HEAD), 0) // 2
        m = None
        for j in range(GROUP):
            part = jnp.dot(p, vbuf[slot, j], preferred_element_type=F32)
            m = part if m is None else jnp.where(owner == j, part, m)
        ma[pl.ds(pl.multiple_of(g * 8, 8), 8), :] = m[:, :HALF]
        mb[pl.ds(pl.multiple_of(g * 8, 8), 8), :] = m[:, HALF:]
        for copy in write_copies(g, slot):
            copy.start()

        @pl.when(g >= 1)
        def _():
            before = lax.rem(g + SLOTS - 1, SLOTS)
            for copy in write_copies(g - 1, before):
                copy.wait()

            @pl.when(g + SLOTS - 1 < groups)
            def _():
                read(g + SLOTS - 1, before)
        return carry

    lax.fori_loop(0, groups, step, 0)

    mixed = jnp.concatenate([ref[pl.ds(h, ROWS, stride=2), :] for h in range(2) for ref in (ma, mb)], axis=1).astype(BF16)
    weights[3].wait()
    for c in range(D // CHUNK):
        o_ref[c] = jnp.dot(mixed, wo[:, c * CHUNK:(c + 1) * CHUNK], preferred_element_type=F32).astype(BF16)
    for copy in write_copies(groups - 1, (groups - 1) % SLOTS):
        copy.wait()


def mlp_kernel(layer, x_hbm, o_hbm, gain_hbm, wg_hbm, wu_hbm, wd_hbm, out_ref,
               x, gain, wg, wu, wd, h, osend, ohalf, orecv1, orecv2, fsend, fhalf, frecv1, frecv2, total,
               small_sem, g_sem, u_sem, d_sem, os1, or1, os2, or2, fs1, fr1, fs2, fr2):
    chunks = D // CHUNK
    me = lax.axis_index("tp")
    chip, core = me // 2, lax.rem(me, 2)
    partner = chip * 2 + (1 - core)
    across = (1 - chip) * 2 + core

    small = [pltpu.make_async_copy(s, d, small_sem.at[i]) for i, (s, d) in enumerate(
        ((o_hbm, osend), (x_hbm, x), (gain_hbm.at[layer], gain)))]
    for copy in small:
        copy.start()
    cols = [pl.ds(c * CHUNK, CHUNK) for c in range(chunks)]
    gates = [pltpu.make_async_copy(wg_hbm.at[layer, :, cols[c]], wg.at[c], g_sem.at[c]) for c in range(chunks)]
    ups = [pltpu.make_async_copy(wu_hbm.at[layer, :, cols[c]], wu.at[c], u_sem.at[c]) for c in range(chunks)]
    downs = [pltpu.make_async_copy(wd_hbm.at[layer, :, cols[c]], wd.at[c], d_sem.at[c]) for c in range(chunks)]
    for c in range(chunks):
        gates[c].start()
        ups[c].start()
    for c in range(chunks):
        downs[c].start()

    barrier = pltpu.get_barrier_semaphore()
    for peer in (partner, across):
        pl.semaphore_signal(barrier, inc=1, device_id={"tp": peer}, device_id_type=pl.DeviceIdType.MESH)
    pl.semaphore_wait(barrier, 2)

    def remote(src, dst, send, recv, c, peer):
        return pltpu.make_async_remote_copy(src_ref=src.at[c], dst_ref=dst.at[c], send_sem=send.at[c], recv_sem=recv.at[c],
                                            device_id={"tp": peer}, device_id_type=pl.DeviceIdType.MESH)

    def to_partner(c, bufs):
        return remote(bufs[0], bufs[2], bufs[4], bufs[5], c, partner)

    def to_across(c, bufs):
        return remote(bufs[1], bufs[3], bufs[6], bufs[7], c, across)

    def relay(c, bufs):
        to_partner(c, bufs).wait_recv()
        bufs[1][c] = (bufs[0][c].astype(F32) + bufs[2][c].astype(F32)).astype(BF16)
        to_across(c, bufs).start()

    def finish(c, bufs):
        to_across(c, bufs).wait_recv()
        total[:, c * CHUNK:(c + 1) * CHUNK] = bufs[1][c].astype(F32) + bufs[3][c].astype(F32)

    def drain(bufs):
        for c in range(chunks):
            to_partner(c, bufs).wait_send()
            to_across(c, bufs).wait_send()

    obufs = (osend, ohalf, orecv1, orecv2, os1, or1, os2, or2)
    fbufs = (fsend, fhalf, frecv1, frecv2, fs1, fr1, fs2, fr2)

    small[0].wait()
    for c in range(chunks):
        to_partner(c, obufs).start()
    for c in range(chunks):
        relay(c, obufs)
    for copy in small[1:]:
        copy.wait()
    for c in range(chunks):
        finish(c, obufs)
    x1 = (x[...].astype(F32) + normed(total[...], gain[1:2, :]).astype(F32)).astype(BF16)
    x[...] = x1
    a = normed(x1.astype(F32), gain[2:3, :])

    for c in range(chunks):
        gates[c].wait()
        gate = jnp.dot(a, wg[c], preferred_element_type=F32)
        ups[c].wait()
        up = jnp.dot(a, wu[c], preferred_element_type=F32)
        h[:, c * CHUNK:(c + 1) * CHUNK] = (jax.nn.gelu(gate, approximate=True) * up).astype(BF16)
    act = h[...]
    for c in range(chunks):
        downs[c].wait()
        fsend[c] = jnp.dot(act, wd[c], preferred_element_type=F32).astype(BF16)
        to_partner(c, fbufs).start()
        if c >= 2:
            relay(c - 2, fbufs)
    for c in range(chunks - 2, chunks):
        relay(c, fbufs)
    for c in range(chunks):
        finish(c, fbufs)
    out_ref[...] = (x[...].astype(F32) + normed(total[...], gain[3:4, :]).astype(F32)).astype(BF16)
    drain(obufs)
    drain(fbufs)


def in_hbm(value):
    return pltpu.with_memory_space_constraint(value, pltpu.HBM)


def attn_call(layer, masked, pos, x, gains, freq, wq, wk, wv, wo, kc, vc):
    n = kc.shape[1]
    dma = pltpu.SemaphoreType.DMA
    any_spec = pl.BlockSpec(memory_space=pl.ANY)
    return pl.pallas_call(
        functools.partial(attn_kernel, layer, masked),
        name=f"attn{layer}",
        out_shape=(jax.ShapeDtypeStruct(kc.shape, BF16), jax.ShapeDtypeStruct(vc.shape, BF16),
                   jax.ShapeDtypeStruct((D // CHUNK, ROWS, CHUNK), BF16)),
        in_specs=[any_spec] * 10,
        out_specs=(pl.BlockSpec(memory_space=pltpu.HBM), pl.BlockSpec(memory_space=pltpu.HBM), pl.BlockSpec(memory_space=pltpu.VMEM)),
        scratch_shapes=[
            pltpu.SMEM((ROWS,), jnp.int32),
            pltpu.VMEM((ROWS, D), BF16), pltpu.VMEM((4, D), F32), pltpu.VMEM((1, HALF), F32),
            pltpu.VMEM((D, 2 * HEAD), BF16), pltpu.VMEM((D, HEAD), BF16), pltpu.VMEM((D, HEAD), BF16), pltpu.VMEM((2 * HEAD, D), BF16),
            pltpu.VMEM((SLOTS, GROUP, n, HEAD), BF16), pltpu.VMEM((SLOTS, GROUP, n, HEAD), BF16),
            pltpu.VMEM((2 * ROWS, HALF), F32), pltpu.VMEM((2 * ROWS, HALF), F32),
            pltpu.VMEM((2 * ROWS, HALF), F32), pltpu.VMEM((2 * ROWS, HALF), F32),
            pltpu.VMEM((ROWS, HEAD), F32), pltpu.VMEM((ROWS, HEAD), F32),
            dma((4,)), dma((4,)), dma((SLOTS,)), dma((SLOTS,)), dma((SLOTS,)), dma((SLOTS,)),
        ],
        compiler_params=pltpu.CompilerParams(vmem_limit_bytes=50 * 2 ** 20),
    )(pos, x, gains, freq, in_hbm(wq), in_hbm(wk), in_hbm(wv), in_hbm(wo), in_hbm(kc), in_hbm(vc))


def mlp_call(layer, x, o, gains, wg, wu, wd):
    dma = pltpu.SemaphoreType.DMA
    chunks = D // CHUNK
    any_spec = pl.BlockSpec(memory_space=pl.ANY)
    wide = pltpu.VMEM((chunks, D, CHUNK), BF16)
    piece = pltpu.VMEM((chunks, ROWS, CHUNK), BF16)
    return pl.pallas_call(
        functools.partial(mlp_kernel, layer),
        name=f"mlp{layer}",
        out_shape=jax.ShapeDtypeStruct((ROWS, D), BF16),
        in_specs=[any_spec] * 6,
        out_specs=pl.BlockSpec(memory_space=pltpu.VMEM),
        scratch_shapes=[
            pltpu.VMEM((ROWS, D), BF16), pltpu.VMEM((4, D), F32), wide, wide, wide, pltpu.VMEM((ROWS, D), BF16),
            piece, piece, piece, piece, piece, piece, piece, piece, pltpu.VMEM((ROWS, D), F32),
            dma((3,)), dma((chunks,)), dma((chunks,)), dma((chunks,)),
        ] + [dma((chunks,))] * 8,
        compiler_params=pltpu.CompilerParams(collective_id=layer, has_side_effects=True, vmem_limit_bytes=50 * 2 ** 20),
    )(x, o, gains, in_hbm(wg), in_hbm(wu), in_hbm(wd))


def decode_step(hidden, positions, k_local, v_local, k_global, v_global, w_query, w_key, w_value, w_out, w_gate, w_up, w_down, norm_scale):
    freq = jnp.asarray((ROPE_BASE ** (-2.0 * np.arange(HALF) / HEAD)).astype(np.float32).reshape(1, HALF))

    def flat(cache):
        return cache.reshape(cache.shape[0], cache.shape[1], HEAD)

    outs = []
    x = hidden
    for layer, (k, v) in enumerate(((k_local, v_local), (k_global, v_global))):
        k_new, v_new, o = attn_call(layer, layer == 1, positions, x, norm_scale, freq, w_query, w_key, w_value, w_out, flat(k), flat(v))
        x = mlp_call(layer, x, o, norm_scale, w_gate, w_up, w_down)
        outs += [k_new.reshape(k.shape), v_new.reshape(v.shape)]
    return (x, *outs)


def solution(mesh):
    row_spec = P('dp', None)
    cache_spec = P('dp', None, 'tp', None)
    col_split = P(None, None, 'tp')
    row_split = P(None, 'tp', None)
    in_specs = (row_spec, P('dp'), cache_spec, cache_spec, cache_spec, cache_spec, col_split, col_split, col_split, row_split, col_split, col_split, row_split, P())
    out_specs = (row_spec, cache_spec, cache_spec, cache_spec, cache_spec)
    return jax.shard_map(decode_step, mesh=mesh, in_specs=in_specs, out_specs=out_specs, check_vma=False)
```

time: 282 us -> 102 us (0.36)
  waiting for transfers between devices: 105 us -> 0 us
  Pallas kernels: 0 us -> 97.6 us
  matrix products: 84.6 us -> 0 us
  other arithmetic: 61.8 us -> 0 us
  between operations: 13.9 us -> 0.7 us
  local copies, waits for them, and re-layouts: 16.3 us -> 3.75 us
    psum x4 -> x0, waiting for transfers between devices: 104 us -> none  [the longest x2 55.1 us: decoder_layer(): attn_sum = lax.psum(attn_part.astype(jnp.bfloat16), 'tp')]
    pallas_call x0 -> x4, Pallas kernels: none -> 97.6 us  [the longest x2 55.8 us: attn_call(): pl.pallas_call(functools.partial(attn_kernel, layer, masked), name=f'attn...]
    dot_general x16 -> x0, matrix products: 84.6 us -> none  [the longest x2 22.6 us: mlp_part(): return jnp.dot(hidden_act, w_down, preferred_element_type=jnp.float32)]
    select_n x2 -> x0, other arithmetic: 47.9 us -> none  [project_and_store(): jnp.where(slot_hit, key_new.astype(jnp.bfloat16)[:, None], k_cache)]
    dot_general x3 -> x0, local copies, waits for them, and re-layouts: 11.5 us -> none  [project_and_store(): jnp.dot(normed, w_query, preferred_element_type=jnp.float32)]
    reduce_sum x8 -> x0, other arithmetic: 8.61 us -> none  [rms_norm(): jnp.mean(values_f32 * values_f32, axis=-1, keepdims=True) + NORM_EPS]
  transfers between devices with their start and end apart: 4 -> 0, of which waited for: 4 -> 0; matrix products, arithmetic and copies ran while one was open for 1% -> 0% of each run, Pallas kernels for 0% -> 0%
where the time goes in v1:
time: 102 us
  Pallas kernels  97.6 us (96%)
  local copies, waits for them, and re-layouts  3.75 us (4%)
    pallas_call x2, Pallas kernels, attn_call(): pl.pallas_call(functools.partial(attn_kernel, layer, masked), name=f'attn...  55.8 us
    pallas_call x2, Pallas kernels, mlp_call(): pl.pallas_call(functools.partial(mlp_kernel, layer), name=f'mlp{layer}',...  41.9 us
    unnamed x13, local copies, waits for them, and re-layouts  3.75 us

profile of v1, /device:TPU:0, one launch (start us, length us, event | category | flops | bytes accessed | tf_op | source)
XLA Modules:
  0.0 102.1 jit_solution(3744512941778004472)
XLA Ops:
  0.6 0.0 copy-start
  0.6 0.9 copy-done
  1.5 0.0 copy-start.2
  1.5 0.9 copy-done.2
  2.4 0.0 copy-start.3
  2.4 0.7 copy-done.3
  3.1 0.0 copy-start.4
  3.1 0.7 copy-done.4
  3.7 0.0 copy-start.1
  3.7 20.1 %attn0.1 = (bf16[24,1024,256]{2,1,0:T(8,128)(2,1)}, bf16[24,1024,256]{2,1,0:T(8,128)(2,1)}, bf16[5,24,512]{2,1,0:T(8,128)(2,1)S(1)}) custom-call(s32[24]{0:T(128)S(1)} %copy-done.3, bf16[24,2560]{1,0:T(8,128)(2,1)S(1)} %copy-done.2, f32[2,4,2560]{2,1,0:T(4,128)S(1)} %copy-done, f32[1,128]{1,0:T(1,128)S(1)} %copy-done.4, bf16[2,2560,512]{2,1,0:T(8,128)(2,1)} %wq_hbm.3, ...), custom_call_target="tpu_custom_call" | custom-call | tf_op jit(solution)/shard_map/attn0/pallas_call | solution.py:248
  23.9 0.0 copy-done.1
  23.9 0.0 copy-start.5
  23.9 22.3 %mlp0.1.x_hbm = bf16[24,2560]{1,0:T(8,128)(2,1)S(1)} custom-call(bf16[24,2560]{1,0:T(8,128)(2,1)S(1)} %copy-done.2, bf16[5,24,512]{2,1,0:T(8,128)(2,1)S(1)} %get-tuple-element.11.o_hbm, f32[2,4,2560]{2,1,0:T(4,128)S(1)} %copy-done.1, bf16[2,2560,2560]{2,1,0:T(8,128)(2,1)} %wg_hbm.3, bf16[2,2560,2560]{2,1,0:T(8,128)(2,1)} %wu_hbm.3, bf16[2,2560,2560]{2,1,0:T(8,128)(2,1)} %wd_hbm.3), custom_call_target="tpu_custom_call" | custom-call | tf_op jit(solution)/shard_map/mlp0/pallas_call | solution.py:275
  46.2 0.0 copy-done.5
  46.2 35.6 %attn1.1 = (bf16[24,2048,256]{2,1,0:T(8,128)(2,1)}, bf16[24,2048,256]{2,1,0:T(8,128)(2,1)}, bf16[5,24,512]{2,1,0:T(8,128)(2,1)S(1)}) custom-call(s32[24]{0:T(128)S(1)} %copy-done.3, bf16[24,2560]{1,0:T(8,128)(2,1)S(1)} %mlp0.1.x_hbm, f32[2,4,2560]{2,1,0:T(4,128)S(1)} %copy-done.1, f32[1,128]{1,0:T(1,128)S(1)} %copy-done.5, bf16[2,2560,512]{2,1,0:T(8,128)(2,1)} %wq_hbm.3, ...), custom_call_target="tpu_custom_call" | custom-call | tf_op jit(solution)/shard_map/attn1/pallas_call | solution.py:248
  81.9 19.5 %mlp1.1 = bf16[24,2560]{1,0:T(8,128)(2,1)S(1)} custom-call(bf16[24,2560]{1,0:T(8,128)(2,1)S(1)} %mlp0.1.x_hbm, bf16[5,24,512]{2,1,0:T(8,128)(2,1)S(1)} %get-tuple-element.12.o_hbm, f32[2,4,2560]{2,1,0:T(4,128)S(1)} %copy-done.1, bf16[2,2560,2560]{2,1,0:T(8,128)(2,1)} %wg_hbm.3, bf16[2,2560,2560]{2,1,0:T(8,128)(2,1)} %wu_hbm.3, bf16[2,2560,2560]{2,1,0:T(8,128)(2,1)} %wd_hbm.3), custom_call_target="tpu_custom_call" | custom-call | tf_op jit(solution)/shard_map/mlp1/pallas_call | solution.py:275
  101.4 0.7 copy.25
Async XLA Ops:
  0.6 0.9 copy-start
  1.5 0.9 copy-start.2
  2.4 0.7 copy-start.3
  3.1 0.7 copy-start.4
  3.7 20.2 %copy-start.1 = (f32[2,4,2560]{2,1,0:T(4,128)S(1)}, f32[2,4,2560]{2,1,0:T(4,128)}, u32[]{:S(2)}) copy-start(f32[2,4,2560]{2,1,0:T(4,128)} %gain_hbm.7) | copy-start | bytes 245764
  23.9 22.3 %copy-start.5 = (f32[1,128]{1,0:T(1,128)S(1)}, f32[1,128]{1,0:T(1,128)}, u32[]{:S(2)}) copy-start(f32[1,128]{1,0:T(1,128)} %constant.2.clone.freq_hbm) | copy-start | bytes 1540

commit v2 on v0

v2 whole, which is shorter than its diff:
```python
import functools

import jax
import jax.numpy as jnp
import numpy as np
from jax import lax
from jax.experimental import pallas as pl
from jax.experimental.pallas import tpu as pltpu
from jax.sharding import PartitionSpec as P

SOFT_CAP = 50.0
NORM_EPS = 1e-6
ROPE_BASE = 10000.0
ROWS = 24
D = 2560
HEAD = 256
HALF = 128
GROUP = 4
CHUNK = 512
SIDE = D // 2
MIB = 2 ** 20
F32 = jnp.float32
BF16 = jnp.bfloat16


def normed(values, gain_row):
    inv_rms = lax.rsqrt(jnp.mean(values * values, axis=-1, keepdims=True) + NORM_EPS)
    return (values * inv_rms * (1.0 + gain_row)).astype(BF16)


def rotation(pos, freq):
    row_ids = lax.broadcasted_iota(jnp.int32, (ROWS, HALF), 0)
    pos_rows = jnp.zeros((ROWS, HALF), jnp.int32)
    for b in range(ROWS):
        pos_rows = jnp.where(row_ids == b, pos[b], pos_rows)
    angles = pos_rows.astype(F32) * freq
    return jnp.cos(angles), jnp.sin(angles)


def rotate(t, cos_part, sin_part):
    first, second = t[:, :HALF], t[:, HALF:]
    return first * cos_part - second * sin_part, second * cos_part + first * sin_part


def store_queries(q, cos_part, sin_part, qa, qb):
    for h in range(2):
        first, second = rotate(q[:, h * HEAD:(h + 1) * HEAD], cos_part, sin_part)
        qa[pl.ds(h, ROWS, stride=2), :] = first
        qb[pl.ds(h, ROWS, stride=2), :] = second


def store_key(k, cos_part, sin_part, knew):
    first, second = rotate(k, cos_part, sin_part)
    knew[:, :HALF] = first
    knew[:, HALF:] = second


def patch(buf, j, row, b, new):
    base = pl.multiple_of((row // 16) * 16, 16)
    tile = buf[j, pl.ds(base, 16), :].astype(F32)
    hit = lax.broadcasted_iota(jnp.int32, (16, HEAD), 0) == row - base
    fresh = jnp.broadcast_to(new[pl.ds(b, 1), :], (16, HEAD))
    buf[j, pl.ds(base, 16), :] = jnp.where(hit, fresh, tile).astype(BF16)


def attend_group(masked, g, pos, kref, vref, wait_k, wait_v, qa, qb, ma, mb, knew, vnew):
    n = kref.shape[1]
    rows8 = pl.ds(g * 8 if isinstance(g, int) else pl.multiple_of(g * 8, 8), 8)
    wait_k()
    for j in range(GROUP):
        b = g * GROUP + j
        patch(kref, j, lax.rem(pos[b], n), b, knew)
    q8 = jnp.concatenate([qa[rows8, :], qb[rows8, :]], axis=1).astype(BF16)
    owner = lax.broadcasted_iota(jnp.int32, (8, n), 0) // 2
    s = None
    for j in range(GROUP):
        part = lax.dot_general(q8, kref[j], (((1,), (1,)), ((), ())), preferred_element_type=F32)
        s = part if s is None else jnp.where(owner == j, part, s)
    e = jnp.exp(SOFT_CAP * jnp.tanh(s * (HEAD ** -0.5 / SOFT_CAP)))
    if masked:
        limit_rows = lax.broadcasted_iota(jnp.int32, (8, 1), 0) // 2
        limit = jnp.zeros((8, 1), jnp.int32)
        for j in range(GROUP):
            limit = jnp.where(limit_rows == j, pos[g * GROUP + j], limit)
        e = jnp.where(lax.broadcasted_iota(jnp.int32, (8, n), 1) <= limit, e, 0.0)
    p = (e / jnp.sum(e, axis=-1, keepdims=True)).astype(BF16)
    wait_v()
    for j in range(GROUP):
        b = g * GROUP + j
        patch(vref, j, lax.rem(pos[b], n), b, vnew)
    owner = lax.broadcasted_iota(jnp.int32, (8, HEAD), 0) // 2
    m = None
    for j in range(GROUP):
        part = jnp.dot(p, vref[j], preferred_element_type=F32)
        m = part if m is None else jnp.where(owner == j, part, m)
    ma[rows8, :] = m[:, :HALF]
    mb[rows8, :] = m[:, HALF:]


def project_out(ma, mb, wo, o_ref):
    mixed = jnp.concatenate([ref[pl.ds(h, ROWS, stride=2), :] for h in range(2) for ref in (ma, mb)], axis=1).astype(BF16)
    for c in range(2):
        o_ref[c] = jnp.dot(mixed, wo[:, c * SIDE:(c + 1) * SIDE], preferred_element_type=F32).astype(BF16)


def group_rows(ref, g):
    return ref.at[pl.ds(g * GROUP, GROUP)]


def local_kernel(pos_hbm, x_hbm, gain_hbm, freq_hbm, wq_hbm, wk_hbm, wv_hbm, wo_hbm, kc_hbm, vc_hbm,
                 ko_hbm, vo_hbm, o_ref, cos_ref, sin_ref,
                 pos, x, gain, freq, wq, wk, wv, wo, kbuf, vbuf, qa, qb, ma, mb, knew, vnew,
                 small_sem, w_sem, kr_sem, vr_sem, kw_sem, vw_sem):
    groups = ROWS // GROUP
    small = [pltpu.make_async_copy(s, d, small_sem.at[i]) for i, (s, d) in enumerate(
        ((x_hbm, x), (gain_hbm.at[0], gain), (pos_hbm, pos), (freq_hbm, freq)))]
    weights = [pltpu.make_async_copy(s.at[0], d, w_sem.at[i]) for i, (s, d) in enumerate(
        ((wq_hbm, wq), (wk_hbm, wk), (wv_hbm, wv), (wo_hbm, wo)))]

    def k_read(g):
        return pltpu.make_async_copy(group_rows(kc_hbm, g), kbuf.at[g], kr_sem.at[g])

    def v_read(g):
        return pltpu.make_async_copy(group_rows(vc_hbm, g), vbuf.at[g], vr_sem.at[g])

    def writes(g):
        return (pltpu.make_async_copy(kbuf.at[g], group_rows(ko_hbm, g), kw_sem.at[g]),
                pltpu.make_async_copy(vbuf.at[g], group_rows(vo_hbm, g), vw_sem.at[g]))

    for copy in small + weights[:3]:
        copy.start()
    for g in range(groups):
        k_read(g).start()
        v_read(g).start()
    weights[3].start()

    for copy in small:
        copy.wait()
    cos_part, sin_part = rotation(pos, freq[...])
    cos_ref[...] = cos_part
    sin_ref[...] = sin_part
    a = normed(x[...].astype(F32), gain[0:1, :])
    weights[0].wait()
    store_queries(jnp.dot(a, wq[...], preferred_element_type=F32), cos_part, sin_part, qa, qb)
    weights[1].wait()
    store_key(jnp.dot(a, wk[...], preferred_element_type=F32), cos_part, sin_part, knew)
    weights[2].wait()
    vnew[...] = jnp.dot(a, wv[...], preferred_element_type=F32)

    def step(g, carry):
        attend_group(False, g, pos, kbuf.at[g], vbuf.at[g], lambda: k_read(g).wait(), lambda: v_read(g).wait(), qa, qb, ma, mb, knew, vnew)
        for copy in writes(g):
            copy.start()
        return carry

    lax.fori_loop(0, groups, step, 0)
    weights[3].wait()
    project_out(ma, mb, wo, o_ref)
    for g in range(groups):
        for copy in writes(g):
            copy.wait()


def global_kernel(pos_hbm, a_ref, cos_ref, sin_ref, wq, wk, wv, wo, _k_first, _v_first, kc_hbm, vc_hbm,
                  ko_hbm, vo_hbm, o_ref, kfirst, vfirst,
                  pos, kbuf, vbuf, qa, qb, ma, mb, knew, vnew,
                  pos_sem, kr_sem, vr_sem, kw_sem, vw_sem):
    groups = ROWS // GROUP
    pos_copy = pltpu.make_async_copy(pos_hbm, pos, pos_sem)

    def k_read(g):
        return pltpu.make_async_copy(group_rows(kc_hbm, g), kbuf.at[g - 1], kr_sem.at[g - 1])

    def v_read(g):
        return pltpu.make_async_copy(group_rows(vc_hbm, g), vbuf.at[g - 1], vr_sem.at[g - 1])

    def writes(g, k, v):
        return (pltpu.make_async_copy(k, group_rows(ko_hbm, g), kw_sem.at[g]),
                pltpu.make_async_copy(v, group_rows(vo_hbm, g), vw_sem.at[g]))

    pos_copy.start()
    for g in range(1, groups):
        k_read(g).start()
        v_read(g).start()
    cos_part, sin_part = cos_ref[...], sin_ref[...]
    a = a_ref[...]
    store_queries(jnp.dot(a, wq[...], preferred_element_type=F32), cos_part, sin_part, qa, qb)
    store_key(jnp.dot(a, wk[...], preferred_element_type=F32), cos_part, sin_part, knew)
    vnew[...] = jnp.dot(a, wv[...], preferred_element_type=F32)
    pos_copy.wait()

    attend_group(True, 0, pos, kfirst, vfirst, lambda: None, lambda: None, qa, qb, ma, mb, knew, vnew)
    for copy in writes(0, kfirst, vfirst):
        copy.start()

    def step(g, carry):
        k, v = kbuf.at[g - 1], vbuf.at[g - 1]
        attend_group(True, g, pos, k, v, lambda: k_read(g).wait(), lambda: v_read(g).wait(), qa, qb, ma, mb, knew, vnew)
        for copy in writes(g, k, v):
            copy.start()
        return carry

    lax.fori_loop(1, groups, step, 0)
    project_out(ma, mb, wo, o_ref)
    for copy in writes(0, kfirst, vfirst):
        copy.wait()
    for g in range(1, groups):
        for copy in writes(g, kbuf.at[g - 1], vbuf.at[g - 1]):
            copy.wait()


def mlp_kernel(layer, *refs):
    n_in, n_out = (12, 8) if layer == 0 else (6, 1)
    x_hbm, o_ref, gain_hbm, wg_hbm, wu_hbm, wd_hbm = refs[:6]
    outs = refs[n_in:n_in + n_out]
    (x, gain, wg, wu, wd, h, osend, ohalf, orecv1, orecv2, osum, fsend, fhalf, frecv1, frecv2, total,
     small_sem, g_sem, u_sem, d_sem, ahead_sem, o_send, o_recv, fs1, fr1, fs2, fr2) = refs[n_in + n_out:]
    out_ref = outs[0]
    chunks = D // CHUNK
    me = lax.axis_index("tp")
    chip, core = me // 2, lax.rem(me, 2)
    partner = chip * 2 + (1 - core)
    across = (1 - chip) * 2 + core

    small = [pltpu.make_async_copy(s, d, small_sem.at[i]) for i, (s, d) in enumerate(
        ((o_ref, osend), (x_hbm, x), (gain_hbm, gain)))]
    cols = [pl.ds(c * CHUNK, CHUNK) for c in range(chunks)]
    gates = [pltpu.make_async_copy(wg_hbm.at[layer, :, cols[c]], wg.at[c], g_sem.at[c]) for c in range(chunks)]
    ups = [pltpu.make_async_copy(wu_hbm.at[layer, :, cols[c]], wu.at[c], u_sem.at[c]) for c in range(chunks)]
    downs = [pltpu.make_async_copy(wd_hbm.at[layer, :, cols[c]], wd.at[c], d_sem.at[c]) for c in range(chunks)]
    for copy in small:
        copy.start()
    for c in range(chunks):
        gates[c].start()
        ups[c].start()
    for c in range(chunks):
        downs[c].start()
    ahead = []
    if layer == 0:
        wq_hbm, wk_hbm, wv_hbm, wo_hbm, kc_hbm, vc_hbm = refs[6:12]
        sources = [w.at[1] for w in (wq_hbm, wk_hbm, wv_hbm, wo_hbm)] + [group_rows(kc_hbm, 0), group_rows(vc_hbm, 0)]
        ahead = [pltpu.make_async_copy(s, d, ahead_sem.at[i]) for i, (s, d) in enumerate(zip(sources, outs[2:]))]
        for copy in ahead:
            copy.start(priority=1)

    barrier = pltpu.get_barrier_semaphore()
    for peer in (partner, across):
        pl.semaphore_signal(barrier, inc=1, device_id={"tp": peer}, device_id_type=pl.DeviceIdType.MESH)
    pl.semaphore_wait(barrier, 2)

    def remote(src, dst, send, recv, peer):
        return pltpu.make_async_remote_copy(src_ref=src, dst_ref=dst, send_sem=send, recv_sem=recv,
                                            device_id={"tp": peer}, device_id_type=pl.DeviceIdType.MESH)

    o_copies = (remote(osend.at[1 - core], orecv1, o_send.at[0], o_recv.at[0], partner),
                remote(ohalf, orecv2, o_send.at[1], o_recv.at[1], across),
                remote(osum.at[core], osum.at[core], o_send.at[2], o_recv.at[2], partner))
    small[0].wait()
    o_copies[0].start()
    for copy in small[1:]:
        copy.wait()
    o_copies[0].wait_recv()
    ohalf[...] = (osend[core].astype(F32) + orecv1[...].astype(F32)).astype(BF16)
    o_copies[1].start()
    o_copies[1].wait_recv()
    osum[core] = (ohalf[...].astype(F32) + orecv2[...].astype(F32)).astype(BF16)
    o_copies[2].start()
    o_copies[2].wait_recv()
    o_sum = jnp.concatenate([osum[0], osum[1]], axis=1).astype(F32)
    x1 = (x[...].astype(F32) + normed(o_sum, gain[layer, 1:2, :]).astype(F32)).astype(BF16)
    x[...] = x1
    a = normed(x1.astype(F32), gain[layer, 2:3, :])

    for c in range(chunks):
        gates[c].wait()
        gate = jnp.dot(a, wg[c], preferred_element_type=F32)
        ups[c].wait()
        up = jnp.dot(a, wu[c], preferred_element_type=F32)
        h[:, c * CHUNK:(c + 1) * CHUNK] = (jax.nn.gelu(gate, approximate=True) * up).astype(BF16)
    act = h[...]

    def to_partner(c):
        return remote(fsend.at[c], frecv1.at[c], fs1.at[c], fr1.at[c], partner)

    def to_across(c):
        return remote(fhalf.at[c], frecv2.at[c], fs2.at[c], fr2.at[c], across)

    def relay(c):
        to_partner(c).wait_recv()
        fhalf[c] = (fsend[c].astype(F32) + frecv1[c].astype(F32)).astype(BF16)
        to_across(c).start()

    for c in range(chunks):
        downs[c].wait()
        fsend[c] = jnp.dot(act, wd[c], preferred_element_type=F32).astype(BF16)
        to_partner(c).start()
        if c >= 3:
            relay(c - 3)
    for c in range(chunks - 3, chunks):
        relay(c)
    squares = jnp.zeros((ROWS, HALF), F32)
    for c in range(chunks):
        to_across(c).wait_recv()
        piece = fhalf[c].astype(F32) + frecv2[c].astype(F32)
        total[:, c * CHUNK:(c + 1) * CHUNK] = piece
        for i in range(CHUNK // HALF):
            lane_block = piece[:, i * HALF:(i + 1) * HALF]
            squares = squares + lane_block * lane_block
    inv_rms = lax.rsqrt(jnp.sum(squares, axis=-1, keepdims=True) / D + NORM_EPS)
    branch = (total[...] * inv_rms * (1.0 + gain[layer, 3:4, :])).astype(BF16)
    x2 = (x[...].astype(F32) + branch.astype(F32)).astype(BF16)
    out_ref[...] = x2
    if layer == 0:
        outs[1][...] = normed(x2.astype(F32), gain[1, 0:1, :])
    for copy in o_copies:
        copy.wait_send()
    for c in range(chunks):
        to_partner(c).wait_send()
        to_across(c).wait_send()
    for copy in ahead:
        copy.wait()


def in_hbm(value):
    return pltpu.with_memory_space_constraint(value, pltpu.HBM)


def in_vmem(value):
    return pltpu.with_memory_space_constraint(value, pltpu.VMEM)


ANY = pl.BlockSpec(memory_space=pl.ANY)
IN_HBM = pl.BlockSpec(memory_space=pltpu.HBM)
IN_VMEM = pl.BlockSpec(memory_space=pltpu.VMEM)
DMA = pltpu.SemaphoreType.DMA


def head_scratch():
    return [pltpu.VMEM((2 * ROWS, HALF), F32)] * 4 + [pltpu.VMEM((ROWS, HEAD), F32)] * 2


def local_call(pos, x, gains, freq, wq, wk, wv, wo, kc, vc):
    groups, n = ROWS // GROUP, kc.shape[1]
    table = pltpu.VMEM((ROWS, HALF), F32)
    return pl.pallas_call(
        local_kernel,
        name="local_attention",
        out_shape=(jax.ShapeDtypeStruct(kc.shape, BF16), jax.ShapeDtypeStruct(vc.shape, BF16),
                   pltpu.VMEM((2, ROWS, SIDE), BF16), table, table),
        in_specs=[ANY] * 10,
        out_specs=(IN_HBM, IN_HBM, IN_VMEM, IN_VMEM, IN_VMEM),
        scratch_shapes=[
            pltpu.SMEM((ROWS,), jnp.int32),
            pltpu.VMEM((ROWS, D), BF16), pltpu.VMEM((4, D), F32), pltpu.VMEM((1, HALF), F32),
            pltpu.VMEM((D, 2 * HEAD), BF16), pltpu.VMEM((D, HEAD), BF16), pltpu.VMEM((D, HEAD), BF16), pltpu.VMEM((2 * HEAD, D), BF16),
            pltpu.VMEM((groups, GROUP, n, HEAD), BF16), pltpu.VMEM((groups, GROUP, n, HEAD), BF16),
        ] + head_scratch() + [DMA((4,)), DMA((4,))] + [DMA((groups,))] * 4,
        compiler_params=pltpu.CompilerParams(vmem_limit_bytes=40 * MIB),
    )(*[in_hbm(v) for v in (pos, x, gains, freq, wq, wk, wv, wo, kc, vc)])


def global_call(pos, a, cos_part, sin_part, ahead, kc, vc):
    groups, n = ROWS // GROUP, kc.shape[1]
    first = pltpu.VMEM((GROUP, n, HEAD), BF16)
    return pl.pallas_call(
        global_kernel,
        name="global_attention",
        out_shape=(jax.ShapeDtypeStruct(kc.shape, BF16), jax.ShapeDtypeStruct(vc.shape, BF16),
                   pltpu.VMEM((2, ROWS, SIDE), BF16), first, first),
        in_specs=[ANY] + [IN_VMEM] * 9 + [ANY] * 2,
        out_specs=(IN_HBM, IN_HBM, IN_VMEM, IN_VMEM, IN_VMEM),
        input_output_aliases={8: 3, 9: 4},
        scratch_shapes=[
            pltpu.SMEM((ROWS,), jnp.int32),
            pltpu.VMEM((groups - 1, GROUP, n, HEAD), BF16), pltpu.VMEM((groups - 1, GROUP, n, HEAD), BF16),
        ] + head_scratch() + [DMA(())] + [DMA((groups - 1,))] * 2 + [DMA((groups,))] * 2,
        compiler_params=pltpu.CompilerParams(vmem_limit_bytes=42 * MIB),
    )(in_hbm(pos), *[in_vmem(v) for v in (a, cos_part, sin_part, *ahead)], in_hbm(kc), in_hbm(vc))


def mlp_call(layer, x, o, gains, wg, wu, wd, ahead=()):
    chunks = D // CHUNK
    wide = pltpu.VMEM((chunks, D, CHUNK), BF16)
    piece = pltpu.VMEM((chunks, ROWS, CHUNK), BF16)
    side = pltpu.VMEM((ROWS, SIDE), BF16)
    both = pltpu.VMEM((2, ROWS, SIDE), BF16)
    rows = pltpu.VMEM((ROWS, D), BF16)
    out_shape = [rows]
    if ahead:
        out_shape += [rows] + [pltpu.VMEM(w.shape[1:], BF16) for w in ahead[:4]]
        out_shape += [pltpu.VMEM((GROUP,) + c.shape[1:], BF16) for c in ahead[4:]]
    return pl.pallas_call(
        functools.partial(mlp_kernel, layer),
        name=f"mlp{layer}",
        out_shape=out_shape,
        in_specs=[ANY] * (6 + len(ahead)),
        out_specs=[IN_VMEM] * len(out_shape),
        scratch_shapes=[
            pltpu.VMEM((ROWS, D), BF16), pltpu.VMEM((2, 4, D), F32), wide, wide, wide, pltpu.VMEM((ROWS, D), BF16),
            both, side, side, side, both, piece, piece, piece, piece, pltpu.VMEM((ROWS, D), F32),
            DMA((3,)), DMA((chunks,)), DMA((chunks,)), DMA((chunks,)), DMA((6,)), DMA((3,)), DMA((3,)),
        ] + [DMA((chunks,))] * 4,
        compiler_params=pltpu.CompilerParams(collective_id=layer, has_side_effects=True, vmem_limit_bytes=40 * MIB),
    )(x, in_vmem(o), *[in_hbm(v) for v in (gains, wg, wu, wd) + tuple(ahead)])


def decode_step(hidden, positions, k_local, v_local, k_global, v_global, w_query, w_key, w_value, w_out, w_gate, w_up, w_down, norm_scale):
    freq = jnp.asarray((ROPE_BASE ** (-2.0 * np.arange(HALF) / HEAD)).astype(np.float32).reshape(1, HALF))

    def flat(cache):
        return cache.reshape(cache.shape[0], cache.shape[1], HEAD)

    kg, vg = flat(k_global), flat(v_global)
    kl_new, vl_new, o, cos_part, sin_part = local_call(positions, hidden, norm_scale, freq, w_query, w_key, w_value, w_out, flat(k_local), flat(v_local))
    x, a, *ahead = mlp_call(0, in_hbm(hidden), o, norm_scale, w_gate, w_up, w_down, (w_query, w_key, w_value, w_out, kg, vg))
    kg_new, vg_new, o, _, _ = global_call(positions, a, cos_part, sin_part, ahead, kg, vg)
    (x,) = mlp_call(1, in_vmem(x), o, norm_scale, w_gate, w_up, w_down)
    return (x, kl_new.reshape(k_local.shape), vl_new.reshape(v_local.shape), kg_new.reshape(k_global.shape), vg_new.reshape(v_global.shape))


def solution(mesh):
    row_spec = P('dp', None)
    cache_spec = P('dp', None, 'tp', None)
    col_split = P(None, None, 'tp')
    row_split = P(None, 'tp', None)
    in_specs = (row_spec, P('dp'), cache_spec, cache_spec, cache_spec, cache_spec, col_split, col_split, col_split, row_split, col_split, col_split, row_split, P())
    out_specs = (row_spec, cache_spec, cache_spec, cache_spec, cache_spec)
    return jax.shard_map(decode_step, mesh=mesh, in_specs=in_specs, out_specs=out_specs, check_vma=False)
```

time: 282 us -> 111 us (0.39)
  Pallas kernels: 0 us -> 109 us
  waiting for transfers between devices: 105 us -> 0 us
  matrix products: 84.6 us -> 0 us
  other arithmetic: 61.8 us -> 0 us
  local copies, waits for them, and re-layouts: 16.3 us -> 0.65 us
  between operations: 13.9 us -> 0.66 us
    pallas_call x0 -> x4, Pallas kernels: none -> 109 us  [the longest x2 58.3 us: mlp_call(): pl.pallas_call(functools.partial(mlp_kernel, layer), name=f'mlp{layer}',...]
    psum x4 -> x0, waiting for transfers between devices: 104 us -> none  [the longest x2 55.1 us: decoder_layer(): attn_sum = lax.psum(attn_part.astype(jnp.bfloat16), 'tp')]
    dot_general x16 -> x0, matrix products: 84.6 us -> none  [the longest x2 22.6 us: mlp_part(): return jnp.dot(hidden_act, w_down, preferred_element_type=jnp.float32)]
    select_n x2 -> x0, other arithmetic: 47.9 us -> none  [project_and_store(): jnp.where(slot_hit, key_new.astype(jnp.bfloat16)[:, None], k_cache)]
    dot_general x3 -> x0, local copies, waits for them, and re-layouts: 11.5 us -> none  [project_and_store(): jnp.dot(normed, w_query, preferred_element_type=jnp.float32)]
    reduce_sum x8 -> x0, other arithmetic: 8.61 us -> none  [rms_norm(): jnp.mean(values_f32 * values_f32, axis=-1, keepdims=True) + NORM_EPS]
    unnamed x8 -> x1, local copies, waits for them, and re-layouts: 4.81 us -> 0.65 us
  transfers between devices with their start and end apart: 4 -> 0, of which waited for: 4 -> 0; matrix products, arithmetic and copies ran while one was open for 1% -> 0% of each run, Pallas kernels for 0% -> 0%
where the time goes in v2:
time: 111 us
  Pallas kernels  109 us (98%)
    pallas_call x2, Pallas kernels, mlp_call(): pl.pallas_call(functools.partial(mlp_kernel, layer), name=f'mlp{layer}',...  58.3 us
    pallas_call x1, Pallas kernels, global_call(): pl.pallas_call(global_kernel, name='global_attention', out_shape=(jax.Sha...  31.9 us
    pallas_call x1, Pallas kernels, local_call(): pl.pallas_call(local_kernel, name='local_attention', out_shape=(jax.Shape...  19.3 us

profile of v2, /device:TPU:0, one launch (start us, length us, event | category | flops | bytes accessed | tf_op | source)
XLA Modules:
  0.0 110.8 jit_solution(4029901087340183829)
XLA Ops:
  0.6 19.3 %local_attention.1 = (bf16[24,1024,256]{2,1,0:T(8,128)(2,1)}, bf16[24,1024,256]{2,1,0:T(8,128)(2,1)}, bf16[2,24,1280]{2,1,0:T(8,128)(2,1)S(1)}, f32[24,128]{1,0:T(8,128)S(1)}, f32[24,128]{1,0:T(8,128)S(1)}) custom-call(s32[24]{0:T(128)} %pos_hbm.3, bf16[24,2560]{1,0:T(8,128)(2,1)} %refs_0_.1, f32[2,4,2560]{2,1,0:T(4,128)} %refs_2_.3, ...), custom_call_target="tpu_custom_call" | custom-call | tf_op jit(solution)/shard_map/local_attention/pallas_call | solution.py:345
  19.9 30.4 %mlp0.1 = (bf16[24,2560]{1,0:T(8,128)(2,1)S(1)}, bf16[24,2560]{1,0:T(8,128)(2,1)S(1)}, bf16[2560,512]{1,0:T(8,128)(2,1)S(1)}, bf16[2560,256]{1,0:T(8,128)(2,1)S(...) custom-call(bf16[24,2560]{1,0:T(8,128)(2,1)} %refs_0_.1, ...), custom_call_target="tpu_custom_call" | custom-call | tf_op jit(solution)/shard_map/mlp0/pallas_call | solution.py:392
  50.3 31.9 %global_attention.1 = (bf16[24,2048,256]{2,1,0:T(8,128)(2,1)}, bf16[24,2048,256]{2,1,0:T(8,128)(2,1)}, bf16[2,24,1280]{2,1,0:T(8,128)(2,1)S(1)}, bf16[4,2048,256...) custom-call(s32[24]{0:T(128)} %pos_hbm.3, ...), custom_call_target="tpu_custom_call", output_to_operand_aliasing={{3}: (8, {}), {4}: (9, {})} | custom-call | tf_op jit(solution)/shard_map/global_attention/pallas_call | solution.py:365
  82.2 27.9 %mlp1.1 = bf16[24,2560]{1,0:T(8,128)(2,1)S(1)} custom-call(bf16[24,2560]{1,0:T(8,128)(2,1)S(1)} %get-tuple-element.22.refs_0_, bf16[2,24,1280]{2,1,0:T(8,128)(2,1)S(1)} %get-tuple-element.32.refs_1_, f32[2,4,2560]{2,1,0:T(4,128)} %refs_2_.3, bf16[2,2560,2560]{2,1,0:T(8,128)(2,1)} %refs_3_.3, bf16[2,2560,2560]{2,1,0:T(8,128)(2,1)} %refs_4_.3, ...), custom_call_target="tpu_custom_call" | custom-call | tf_op jit(solution)/shard_map/mlp1/pallas_call | solution.py:392
  110.1 0.7 copy.29

commit v3 on v2

--- a/solution.py
+++ b/solution.py
@@ -19,6 +19,8 @@
 CHUNK = 512
 SIDE = D // 2
 MIB = 2 ** 20
+WIDE = ((0, 1536), (1536, 1024))
+DOWN = ((0, 1280), (1280, 768), (2048, 512))
 F32 = jnp.float32
 BF16 = jnp.bfloat16
 
@@ -108,8 +110,8 @@
 
 
 def local_kernel(pos_hbm, x_hbm, gain_hbm, freq_hbm, wq_hbm, wk_hbm, wv_hbm, wo_hbm, kc_hbm, vc_hbm,
-                 ko_hbm, vo_hbm, o_ref, cos_ref, sin_ref,
-                 pos, x, gain, freq, wq, wk, wv, wo, kbuf, vbuf, qa, qb, ma, mb, knew, vnew,
+                 ko_hbm, vo_hbm, o_ref, cos_ref, sin_ref, x,
+                 pos, gain, freq, wq, wk, wv, wo, kbuf, vbuf, qa, qb, ma, mb, knew, vnew,
                  small_sem, w_sem, kr_sem, vr_sem, kw_sem, vw_sem):
     groups = ROWS // GROUP
     small = [pltpu.make_async_copy(s, d, small_sem.at[i]) for i, (s, d) in enumerate(
@@ -127,12 +129,14 @@
         return (pltpu.make_async_copy(kbuf.at[g], group_rows(ko_hbm, g), kw_sem.at[g]),
                 pltpu.make_async_copy(vbuf.at[g], group_rows(vo_hbm, g), vw_sem.at[g]))
 
-    for copy in small + weights[:3]:
+    for copy in small:
         copy.start()
+    for copy in weights[:3]:
+        copy.start(priority=1)
     for g in range(groups):
-        k_read(g).start()
-        v_read(g).start()
-    weights[3].start()
+        k_read(g).start(priority=1)
+        v_read(g).start(priority=1)
+    weights[3].start(priority=1)
 
     for copy in small:
         copy.wait()
@@ -150,7 +154,7 @@
     def step(g, carry):
         attend_group(False, g, pos, kbuf.at[g], vbuf.at[g], lambda: k_read(g).wait(), lambda: v_read(g).wait(), qa, qb, ma, mb, knew, vnew)
         for copy in writes(g):
-            copy.start()
+            copy.start(priority=1)
         return carry
 
     lax.fori_loop(0, groups, step, 0)
@@ -178,10 +182,14 @@
         return (pltpu.make_async_copy(k, group_rows(ko_hbm, g), kw_sem.at[g]),
                 pltpu.make_async_copy(v, group_rows(vo_hbm, g), vw_sem.at[g]))
 
+    def start_writes(g):
+        for copy in writes(g, kfirst if g == 0 else kbuf.at[g - 1], vfirst if g == 0 else vbuf.at[g - 1]):
+            copy.start(priority=1)
+
     pos_copy.start()
     for g in range(1, groups):
-        k_read(g).start()
-        v_read(g).start()
+        k_read(g).start(priority=1)
+        v_read(g).start(priority=1)
     cos_part, sin_part = cos_ref[...], sin_ref[...]
     a = a_ref[...]
     store_queries(jnp.dot(a, wq[...], preferred_element_type=F32), cos_part, sin_part, qa, qb)
@@ -190,17 +198,23 @@
     pos_copy.wait()
 
     attend_group(True, 0, pos, kfirst, vfirst, lambda: None, lambda: None, qa, qb, ma, mb, knew, vnew)
-    for copy in writes(0, kfirst, vfirst):
-        copy.start()
 
     def step(g, carry):
         k, v = kbuf.at[g - 1], vbuf.at[g - 1]
-        attend_group(True, g, pos, k, v, lambda: k_read(g).wait(), lambda: v_read(g).wait(), qa, qb, ma, mb, knew, vnew)
-        for copy in writes(g, k, v):
-            copy.start()
+
+        def wait_v():
+            v_read(g).wait()
+
+            @pl.when(g == groups - 1)
+            def _():
+                for i in range(groups - 1):
+                    start_writes(i)
+
+        attend_group(True, g, pos, k, v, lambda: k_read(g).wait(), wait_v, qa, qb, ma, mb, knew, vnew)
         return carry
 
     lax.fori_loop(1, groups, step, 0)
+    start_writes(groups - 1)
     project_out(ma, mb, wo, o_ref)
     for copy in writes(0, kfirst, vfirst):
         copy.wait()
@@ -211,37 +225,36 @@
 
 def mlp_kernel(layer, *refs):
     n_in, n_out = (12, 8) if layer == 0 else (6, 1)
-    x_hbm, o_ref, gain_hbm, wg_hbm, wu_hbm, wd_hbm = refs[:6]
+    x_ref, o_ref, gain_hbm, wg_hbm, wu_hbm, wd_hbm = refs[:6]
     outs = refs[n_in:n_in + n_out]
-    (x, gain, wg, wu, wd, h, osend, ohalf, orecv1, orecv2, osum, fsend, fhalf, frecv1, frecv2, total,
+    (x, gain, wg, wu, wd, h, ohalf, orecv1, orecv2, osum, fsend, fhalf, frecv1, frecv2, total,
      small_sem, g_sem, u_sem, d_sem, ahead_sem, o_send, o_recv, fs1, fr1, fs2, fr2) = refs[n_in + n_out:]
     out_ref = outs[0]
-    chunks = D // CHUNK
+    last = len(DOWN)
     me = lax.axis_index("tp")
     chip, core = me // 2, lax.rem(me, 2)
     partner = chip * 2 + (1 - core)
-    across = (1 - chip) * 2 + core
-
-    small = [pltpu.make_async_copy(s, d, small_sem.at[i]) for i, (s, d) in enumerate(
-        ((o_ref, osend), (x_hbm, x), (gain_hbm, gain)))]
-    cols = [pl.ds(c * CHUNK, CHUNK) for c in range(chunks)]
-    gates = [pltpu.make_async_copy(wg_hbm.at[layer, :, cols[c]], wg.at[c], g_sem.at[c]) for c in range(chunks)]
-    ups = [pltpu.make_async_copy(wu_hbm.at[layer, :, cols[c]], wu.at[c], u_sem.at[c]) for c in range(chunks)]
-    downs = [pltpu.make_async_copy(wd_hbm.at[layer, :, cols[c]], wd.at[c], d_sem.at[c]) for c in range(chunks)]
-    for copy in small:
-        copy.start()
-    for c in range(chunks):
-        gates[c].start()
-        ups[c].start()
-    for c in range(chunks):
-        downs[c].start()
+    across = (1 - chip) * 2 + (1 - core)
+    side = lax.rem(chip + core, 2)
+
+    gain_copy = pltpu.make_async_copy(gain_hbm, gain, small_sem)
+    wide_cols = [pl.ds(start, size) for start, size in WIDE]
+    down_cols = [pl.ds(start, size) for start, size in DOWN]
+    gates = [pltpu.make_async_copy(wg_hbm.at[layer, :, d], wg.at[:, d], g_sem.at[i]) for i, d in enumerate(wide_cols)]
+    ups = [pltpu.make_async_copy(wu_hbm.at[layer, :, d], wu.at[:, d], u_sem.at[i]) for i, d in enumerate(wide_cols)]
+    downs = [pltpu.make_async_copy(wd_hbm.at[layer, :, d], wd.at[:, d], d_sem.at[i]) for i, d in enumerate(down_cols)]
     ahead = []
     if layer == 0:
         wq_hbm, wk_hbm, wv_hbm, wo_hbm, kc_hbm, vc_hbm = refs[6:12]
         sources = [w.at[1] for w in (wq_hbm, wk_hbm, wv_hbm, wo_hbm)] + [group_rows(kc_hbm, 0), group_rows(vc_hbm, 0)]
         ahead = [pltpu.make_async_copy(s, d, ahead_sem.at[i]) for i, (s, d) in enumerate(zip(sources, outs[2:]))]
-        for copy in ahead:
+
+    def start_bulk(copies):
+        for copy in copies:
             copy.start(priority=1)
+
+    gain_copy.start()
+    start_bulk((gates[0], ups[0]))
 
     barrier = pltpu.get_barrier_semaphore()
     for peer in (partner, across):
@@ -252,58 +265,62 @@
         return pltpu.make_async_remote_copy(src_ref=src, dst_ref=dst, send_sem=send, recv_sem=recv,
                                             device_id={"tp": peer}, device_id_type=pl.DeviceIdType.MESH)
 
-    o_copies = (remote(osend.at[1 - core], orecv1, o_send.at[0], o_recv.at[0], partner),
+    o_copies = (remote(o_ref.at[1 - side], orecv1, o_send.at[0], o_recv.at[0], partner),
                 remote(ohalf, orecv2, o_send.at[1], o_recv.at[1], across),
-                remote(osum.at[core], osum.at[core], o_send.at[2], o_recv.at[2], partner))
-    small[0].wait()
+                remote(osum.at[side], osum.at[side], o_send.at[2], o_recv.at[2], partner))
     o_copies[0].start()
-    for copy in small[1:]:
-        copy.wait()
+    start_bulk((gates[1], ups[1]))
+    gain_copy.wait()
     o_copies[0].wait_recv()
-    ohalf[...] = (osend[core].astype(F32) + orecv1[...].astype(F32)).astype(BF16)
+    ohalf[...] = (o_ref[side].astype(F32) + orecv1[...].astype(F32)).astype(BF16)
     o_copies[1].start()
     o_copies[1].wait_recv()
-    osum[core] = (ohalf[...].astype(F32) + orecv2[...].astype(F32)).astype(BF16)
+    osum[side] = (ohalf[...].astype(F32) + orecv2[...].astype(F32)).astype(BF16)
     o_copies[2].start()
     o_copies[2].wait_recv()
     o_sum = jnp.concatenate([osum[0], osum[1]], axis=1).astype(F32)
-    x1 = (x[...].astype(F32) + normed(o_sum, gain[layer, 1:2, :]).astype(F32)).astype(BF16)
+    x1 = (x_ref[...].astype(F32) + normed(o_sum, gain[layer, 1:2, :]).astype(F32)).astype(BF16)
     x[...] = x1
     a = normed(x1.astype(F32), gain[layer, 2:3, :])
 
-    for c in range(chunks):
-        gates[c].wait()
-        gate = jnp.dot(a, wg[c], preferred_element_type=F32)
-        ups[c].wait()
-        up = jnp.dot(a, wu[c], preferred_element_type=F32)
-        h[:, c * CHUNK:(c + 1) * CHUNK] = (jax.nn.gelu(gate, approximate=True) * up).astype(BF16)
+    for w, (start, size) in enumerate(WIDE):
+        gates[w].wait()
+        ups[w].wait()
+        start_bulk(downs if w == 0 else ahead)
+        for c in range(start, start + size, CHUNK):
+            gate = jnp.dot(a, wg[:, c:c + CHUNK], preferred_element_type=F32)
+            up = jnp.dot(a, wu[:, c:c + CHUNK], preferred_element_type=F32)
+            h[:, c:c + CHUNK] = (jax.nn.gelu(gate, approximate=True) * up).astype(BF16)
     act = h[...]
 
     def to_partner(c):
-        return remote(fsend.at[c], frecv1.at[c], fs1.at[c], fr1.at[c], partner)
+        d = down_cols[c]
+        return remote(fsend.at[:, d], frecv1.at[:, d], fs1.at[c], fr1.at[c], partner)
 
     def to_across(c):
-        return remote(fhalf.at[c], frecv2.at[c], fs2.at[c], fr2.at[c], across)
+        d = down_cols[c]
+        return remote(fhalf.at[:, d], frecv2.at[:, d], fs2.at[c], fr2.at[c], across)
 
     def relay(c):
+        d = down_cols[c]
         to_partner(c).wait_recv()
-        fhalf[c] = (fsend[c].astype(F32) + frecv1[c].astype(F32)).astype(BF16)
+        fhalf[:, d] = (fsend[:, d].astype(F32) + frecv1[:, d].astype(F32)).astype(BF16)
         to_across(c).start()
 
-    for c in range(chunks):
+    for c in range(last):
         downs[c].wait()
-        fsend[c] = jnp.dot(act, wd[c], preferred_element_type=F32).astype(BF16)
+        fsend[:, down_cols[c]] = jnp.dot(act, wd[:, down_cols[c]], preferred_element_type=F32).astype(BF16)
         to_partner(c).start()
-        if c >= 3:
-            relay(c - 3)
-    for c in range(chunks - 3, chunks):
+        if c >= 1:
+            relay(c - 1)
+    for c in range(last - 1, last):
         relay(c)
     squares = jnp.zeros((ROWS, HALF), F32)
-    for c in range(chunks):
+    for c in range(last):
         to_across(c).wait_recv()
-        piece = fhalf[c].astype(F32) + frecv2[c].astype(F32)
-        total[:, c * CHUNK:(c + 1) * CHUNK] = piece
-        for i in range(CHUNK // HALF):
+        piece = fhalf[:, down_cols[c]].astype(F32) + frecv2[:, down_cols[c]].astype(F32)
+        total[:, down_cols[c]] = piece
+        for i in range(DOWN[c][1] // HALF):
             lane_block = piece[:, i * HALF:(i + 1) * HALF]
             squares = squares + lane_block * lane_block
     inv_rms = lax.rsqrt(jnp.sum(squares, axis=-1, keepdims=True) / D + NORM_EPS)
@@ -314,7 +331,7 @@
         outs[1][...] = normed(x2.astype(F32), gain[1, 0:1, :])
     for copy in o_copies:
         copy.wait_send()
-    for c in range(chunks):
+    for c in range(last):
         to_partner(c).wait_send()
         to_across(c).wait_send()
     for copy in ahead:
@@ -346,12 +363,12 @@
         local_kernel,
         name="local_attention",
         out_shape=(jax.ShapeDtypeStruct(kc.shape, BF16), jax.ShapeDtypeStruct(vc.shape, BF16),
-                   pltpu.VMEM((2, ROWS, SIDE), BF16), table, table),
+                   pltpu.VMEM((2, ROWS, SIDE), BF16), table, table, pltpu.VMEM(x.shape, BF16)),
         in_specs=[ANY] * 10,
-        out_specs=(IN_HBM, IN_HBM, IN_VMEM, IN_VMEM, IN_VMEM),
+        out_specs=(IN_HBM, IN_HBM, IN_VMEM, IN_VMEM, IN_VMEM, IN_VMEM),
         scratch_shapes=[
             pltpu.SMEM((ROWS,), jnp.int32),
-            pltpu.VMEM((ROWS, D), BF16), pltpu.VMEM((4, D), F32), pltpu.VMEM((1, HALF), F32),
+            pltpu.VMEM((4, D), F32), pltpu.VMEM((1, HALF), F32),
             pltpu.VMEM((D, 2 * HEAD), BF16), pltpu.VMEM((D, HEAD), BF16), pltpu.VMEM((D, HEAD), BF16), pltpu.VMEM((2 * HEAD, D), BF16),
             pltpu.VMEM((groups, GROUP, n, HEAD), BF16), pltpu.VMEM((groups, GROUP, n, HEAD), BF16),
         ] + head_scratch() + [DMA((4,)), DMA((4,))] + [DMA((groups,))] * 4,
@@ -379,9 +396,8 @@
 
 
 def mlp_call(layer, x, o, gains, wg, wu, wd, ahead=()):
-    chunks = D // CHUNK
-    wide = pltpu.VMEM((chunks, D, CHUNK), BF16)
-    piece = pltpu.VMEM((chunks, ROWS, CHUNK), BF16)
+    square = pltpu.VMEM((D, D), BF16)
+    full = pltpu.VMEM((ROWS, D), BF16)
     side = pltpu.VMEM((ROWS, SIDE), BF16)
     both = pltpu.VMEM((2, ROWS, SIDE), BF16)
     rows = pltpu.VMEM((ROWS, D), BF16)
@@ -393,15 +409,15 @@
         functools.partial(mlp_kernel, layer),
         name=f"mlp{layer}",
         out_shape=out_shape,
-        in_specs=[ANY] * (6 + len(ahead)),
+        in_specs=[IN_VMEM] * 2 + [ANY] * (4 + len(ahead)),
         out_specs=[IN_VMEM] * len(out_shape),
         scratch_shapes=[
-            pltpu.VMEM((ROWS, D), BF16), pltpu.VMEM((2, 4, D), F32), wide, wide, wide, pltpu.VMEM((ROWS, D), BF16),
-            both, side, side, side, both, piece, piece, piece, piece, pltpu.VMEM((ROWS, D), F32),
-            DMA((3,)), DMA((chunks,)), DMA((chunks,)), DMA((chunks,)), DMA((6,)), DMA((3,)), DMA((3,)),
-        ] + [DMA((chunks,))] * 4,
+            full, pltpu.VMEM((2, 4, D), F32), square, square, square, full,
+            side, side, side, both, full, full, full, full, pltpu.VMEM((ROWS, D), F32),
+            DMA(()), DMA((len(WIDE),)), DMA((len(WIDE),)), DMA((len(DOWN),)), DMA((6,)), DMA((3,)), DMA((3,)),
+        ] + [DMA((len(DOWN),))] * 4,
         compiler_params=pltpu.CompilerParams(collective_id=layer, has_side_effects=True, vmem_limit_bytes=40 * MIB),
-    )(x, in_vmem(o), *[in_hbm(v) for v in (gains, wg, wu, wd) + tuple(ahead)])
+    )(in_vmem(x), in_vmem(o), *[in_hbm(v) for v in (gains, wg, wu, wd) + tuple(ahead)])
 
 
 def decode_step(hidden, positions, k_local, v_local, k_global, v_global, w_query, w_key, w_value, w_out, w_gate, w_up, w_down, norm_scale):
@@ -411,10 +427,10 @@
         return cache.reshape(cache.shape[0], cache.shape[1], HEAD)
 
     kg, vg = flat(k_global), flat(v_global)
-    kl_new, vl_new, o, cos_part, sin_part = local_call(positions, hidden, norm_scale, freq, w_query, w_key, w_value, w_out, flat(k_local), flat(v_local))
-    x, a, *ahead = mlp_call(0, in_hbm(hidden), o, norm_scale, w_gate, w_up, w_down, (w_query, w_key, w_value, w_out, kg, vg))
+    kl_new, vl_new, o, cos_part, sin_part, x = local_call(positions, hidden, norm_scale, freq, w_query, w_key, w_value, w_out, flat(k_local), flat(v_local))
+    x, a, *ahead = mlp_call(0, x, o, norm_scale, w_gate, w_up, w_down, (w_query, w_key, w_value, w_out, kg, vg))
     kg_new, vg_new, o, _, _ = global_call(positions, a, cos_part, sin_part, ahead, kg, vg)
-    (x,) = mlp_call(1, in_vmem(x), o, norm_scale, w_gate, w_up, w_down)
+    (x,) = mlp_call(1, x, o, norm_scale, w_gate, w_up, w_down)
     return (x, kl_new.reshape(k_local.shape), vl_new.reshape(v_local.shape), kg_new.reshape(k_global.shape), vg_new.reshape(v_global.shape))
 
 

time: 111 us -> 86.9 us (0.78)
  Pallas kernels: 109 us -> 85.5 us
    pallas_call x2, Pallas kernels: 58.3 us -> 37.6 us  [mlp_call(): pl.pallas_call(functools.partial(mlp_kernel, layer), name=f'mlp{layer}',...]
    pallas_call x1, Pallas kernels: 31.9 us -> 30.2 us  [global_call(): pl.pallas_call(global_kernel, name='global_attention', out_shape=(jax.Sha...]
    pallas_call x1, Pallas kernels: 19.3 us -> 17.7 us  [local_call(): pl.pallas_call(local_kernel, name='local_attention', out_shape=(jax.Shape...]
where the time goes in v3:
time: 86.9 us
  Pallas kernels  85.5 us (98%)
    pallas_call x2, Pallas kernels, mlp_call(): pl.pallas_call(functools.partial(mlp_kernel, layer), name=f'mlp{layer}',...  37.6 us
    pallas_call x1, Pallas kernels, global_call(): pl.pallas_call(global_kernel, name='global_attention', out_shape=(jax.Sha...  30.2 us
    pallas_call x1, Pallas kernels, local_call(): pl.pallas_call(local_kernel, name='local_attention', out_shape=(jax.Shape...  17.7 us

profile of v3, /device:TPU:0, one launch (start us, length us, event | category | flops | bytes accessed | tf_op | source)
XLA Modules:
  0.0 86.9 jit_solution(16078584635729023193)
XLA Ops:
  0.6 17.7 %local_attention.1 = (bf16[24,1024,256]{2,1,0:T(8,128)(2,1)}, bf16[24,1024,256]{2,1,0:T(8,128)(2,1)}, bf16[2,24,1280]{2,1,0:T(8,128)(2,1)S(1)}, f32[24,128]{1,0:...) custom-call(s32[24]{0:T(128)} %pos_hbm.3, bf16[24,2560]{1,0:T(8,128)(2,1)} %x_hbm.1, ...), custom_call_target="tpu_custom_call" | custom-call | tf_op jit(solution)/shard_map/local_attention/pallas_call | solution.py:362
  18.4 20.3 %mlp0.1 = (bf16[24,2560]{1,0:T(8,128)(2,1)S(1)}, bf16[24,2560]{1,0:T(8,128)(2,1)S(1)}, bf16[2560,512]{1,0:T(8,128)(2,1)S(1)}, bf16[2560,256]{1,0:T(8,128)(2,1)S(...) custom-call(bf16[24,2560]{1,0:T(8,128)(2,1)S(1)} %get-tuple-element., ...), custom_call_target="tpu_custom_call" | custom-call | tf_op jit(solution)/shard_map/mlp0/pallas_call | solution.py:408
  38.6 30.2 %global_attention.1 = (bf16[24,2048,256]{2,1,0:T(8,128)(2,1)}, bf16[24,2048,256]{2,1,0:T(8,128)(2,1)}, bf16[2,24,1280]{2,1,0:T(8,128)(2,1)S(1)}, bf16[4,2048,256...) custom-call(s32[24]{0:T(128)} %pos_hbm.3, ...), custom_call_target="tpu_custom_call", output_to_operand_aliasing={{3}: (8, {}), {4}: (9, {})} | custom-call | tf_op jit(solution)/shard_map/global_attention/pallas_call | solution.py:382
  68.9 17.3 %mlp1.1 = bf16[24,2560]{1,0:T(8,128)(2,1)S(1)} custom-call(bf16[24,2560]{1,0:T(8,128)(2,1)S(1)} %get-tuple-element.24.refs_0_, bf16[2,24,1280]{2,1,0:T(8,128)(2,1)S(1)} %get-tuple-element.34.refs_1_, f32[2,4,2560]{2,1,0:T(4,128)} %refs_2_.3, bf16[2,2560,2560]{2,1,0:T(8,128)(2,1)} %refs_3_.3, bf16[2,2560,2560]{2,1,0:T(8,128)(2,1)} %refs_4_.3, ...), custom_call_target="tpu_custom_call" | custom-call | tf_op jit(solution)/shard_map/mlp1/pallas_call | solution.py:408
  86.2 0.7 copy.29

commit v4 on v3

--- a/solution.py
+++ b/solution.py
@@ -19,6 +19,7 @@
 CHUNK = 512
 SIDE = D // 2
 MIB = 2 ** 20
+WRITES_FROM = 4
 WIDE = ((0, 1536), (1536, 1024))
 DOWN = ((0, 1280), (1280, 768), (2048, 512))
 F32 = jnp.float32
@@ -205,16 +206,20 @@
         def wait_v():
             v_read(g).wait()
 
-            @pl.when(g == groups - 1)
+            @pl.when(g == WRITES_FROM)
             def _():
-                for i in range(groups - 1):
+                for i in range(WRITES_FROM):
                     start_writes(i)
 
         attend_group(True, g, pos, k, v, lambda: k_read(g).wait(), wait_v, qa, qb, ma, mb, knew, vnew)
+
+        @pl.when(g >= WRITES_FROM)
+        def _():
+            for copy in writes(g, k, v):
+                copy.start(priority=1)
         return carry
 
     lax.fori_loop(1, groups, step, 0)
-    start_writes(groups - 1)
     project_out(ma, mb, wo, o_ref)
     for copy in writes(0, kfirst, vfirst):
         copy.wait()

time: 86.9 us -> 85.3 us (0.982)
  Pallas kernels: 85.5 us -> 83.9 us
    pallas_call x1, Pallas kernels: 30.2 us -> 28.6 us  [global_call(): pl.pallas_call(global_kernel, name='global_attention', out_shape=(jax.Sha...]
where the time goes in v4:
time: 85.3 us; the launch traced here: 85.2 us
  Pallas kernels  83.9 us (98%)
    pallas_call x2, Pallas kernels, mlp_call(): pl.pallas_call(functools.partial(mlp_kernel, layer), name=f'mlp{layer}',...  37.6 us
    pallas_call x1, Pallas kernels, global_call(): pl.pallas_call(global_kernel, name='global_attention', out_shape=(jax.Sha...  28.6 us
    pallas_call x1, Pallas kernels, local_call(): pl.pallas_call(local_kernel, name='local_attention', out_shape=(jax.Shape...  17.7 us

profile of v4, /device:TPU:0, one launch (start us, length us, event | category | flops | bytes accessed | tf_op | source)
XLA Modules:
  0.0 85.2 jit_solution(10237021864597581893)
XLA Ops:
  0.6 17.7 %local_attention.1 = (bf16[24,1024,256]{2,1,0:T(8,128)(2,1)}, bf16[24,1024,256]{2,1,0:T(8,128)(2,1)}, bf16[2,24,1280]{2,1,0:T(8,128)(2,1)S(1)}, f32[24,128]{1,0:...) custom-call(s32[24]{0:T(128)} %pos_hbm.3, bf16[24,2560]{1,0:T(8,128)(2,1)} %x_hbm.1, ...), custom_call_target="tpu_custom_call" | custom-call | tf_op jit(solution)/shard_map/local_attention/pallas_call | solution.py:367
  18.4 20.3 %mlp0.1 = (bf16[24,2560]{1,0:T(8,128)(2,1)S(1)}, bf16[24,2560]{1,0:T(8,128)(2,1)S(1)}, bf16[2560,512]{1,0:T(8,128)(2,1)S(1)}, bf16[2560,256]{1,0:T(8,128)(2,1)S(...) custom-call(bf16[24,2560]{1,0:T(8,128)(2,1)S(1)} %get-tuple-element., ...), custom_call_target="tpu_custom_call" | custom-call | tf_op jit(solution)/shard_map/mlp0/pallas_call | solution.py:413
  38.6 28.6 %global_attention.1 = (bf16[24,2048,256]{2,1,0:T(8,128)(2,1)}, bf16[24,2048,256]{2,1,0:T(8,128)(2,1)}, bf16[2,24,1280]{2,1,0:T(8,128)(2,1)S(1)}, bf16[4,2048,256...) custom-call(s32[24]{0:T(128)} %pos_hbm.3, ...), custom_call_target="tpu_custom_call", output_to_operand_aliasing={{3}: (8, {}), {4}: (9, {})} | custom-call | tf_op jit(solution)/shard_map/global_attention/pallas_call | solution.py:387
  67.2 17.3 %mlp1.1 = bf16[24,2560]{1,0:T(8,128)(2,1)S(1)} custom-call(bf16[24,2560]{1,0:T(8,128)(2,1)S(1)} %get-tuple-element.24.refs_0_, bf16[2,24,1280]{2,1,0:T(8,128)(2,1)S(1)} %get-tuple-element.34.refs_1_, f32[2,4,2560]{2,1,0:T(4,128)} %refs_2_.3, bf16[2,2560,2560]{2,1,0:T(8,128)(2,1)} %refs_3_.3, bf16[2,2560,2560]{2,1,0:T(8,128)(2,1)} %refs_4_.3, ...), custom_call_target="tpu_custom_call" | custom-call | tf_op jit(solution)/shard_map/mlp1/pallas_call | solution.py:413
  84.6 0.7 copy.29

commit v5 on v3

--- a/solution.py
+++ b/solution.py
@@ -19,8 +19,9 @@
 CHUNK = 512
 SIDE = D // 2
 MIB = 2 ** 20
-WIDE = ((0, 1536), (1536, 1024))
-DOWN = ((0, 1280), (1280, 768), (2048, 512))
+FIRST = 3
+FF_PART = D // 2
+PIECE = 256
 F32 = jnp.float32
 BF16 = jnp.bfloat16
 
@@ -165,29 +166,25 @@
             copy.wait()
 
 
-def global_kernel(pos_hbm, a_ref, cos_ref, sin_ref, wq, wk, wv, wo, _k_first, _v_first, kc_hbm, vc_hbm,
-                  ko_hbm, vo_hbm, o_ref, kfirst, vfirst,
-                  pos, kbuf, vbuf, qa, qb, ma, mb, knew, vnew,
-                  pos_sem, kr_sem, vr_sem, kw_sem, vw_sem):
+def global_kernel(pos_hbm, a_ref, cos_ref, sin_ref, wq, wk, wv, wo, *refs):
+    kc_hbm, vc_hbm, ko_hbm, vo_hbm, o_ref = refs[2 * FIRST:2 * FIRST + 5]
+    kfirst, vfirst = refs[2 * FIRST + 5:3 * FIRST + 5], refs[3 * FIRST + 5:4 * FIRST + 5]
+    pos, kbuf, vbuf, qa, qb, ma, mb, knew, vnew, pos_sem, kr_sem, vr_sem, kw_sem, vw_sem = refs[4 * FIRST + 5:]
     groups = ROWS // GROUP
     pos_copy = pltpu.make_async_copy(pos_hbm, pos, pos_sem)
 
     def k_read(g):
-        return pltpu.make_async_copy(group_rows(kc_hbm, g), kbuf.at[g - 1], kr_sem.at[g - 1])
+        return pltpu.make_async_copy(group_rows(kc_hbm, g), kbuf.at[g - FIRST], kr_sem.at[g - FIRST])
 
     def v_read(g):
-        return pltpu.make_async_copy(group_rows(vc_hbm, g), vbuf.at[g - 1], vr_sem.at[g - 1])
+        return pltpu.make_async_copy(group_rows(vc_hbm, g), vbuf.at[g - FIRST], vr_sem.at[g - FIRST])
 
     def writes(g, k, v):
         return (pltpu.make_async_copy(k, group_rows(ko_hbm, g), kw_sem.at[g]),
                 pltpu.make_async_copy(v, group_rows(vo_hbm, g), vw_sem.at[g]))
 
-    def start_writes(g):
-        for copy in writes(g, kfirst if g == 0 else kbuf.at[g - 1], vfirst if g == 0 else vbuf.at[g - 1]):
-            copy.start(priority=1)
-
     pos_copy.start()
-    for g in range(1, groups):
+    for g in range(FIRST, groups):
         k_read(g).start(priority=1)
         v_read(g).start(priority=1)
     cos_part, sin_part = cos_ref[...], sin_ref[...]
@@ -197,143 +194,135 @@
     vnew[...] = jnp.dot(a, wv[...], preferred_element_type=F32)
     pos_copy.wait()
 
-    attend_group(True, 0, pos, kfirst, vfirst, lambda: None, lambda: None, qa, qb, ma, mb, knew, vnew)
+    for g in range(FIRST):
+        attend_group(True, g, pos, kfirst[g], vfirst[g], lambda: None, lambda: None, qa, qb, ma, mb, knew, vnew)
+    for g in range(FIRST):
+        for copy in writes(g, kfirst[g], vfirst[g]):
+            copy.start(priority=1)
 
     def step(g, carry):
-        k, v = kbuf.at[g - 1], vbuf.at[g - 1]
-
-        def wait_v():
-            v_read(g).wait()
-
-            @pl.when(g == groups - 1)
-            def _():
-                for i in range(groups - 1):
-                    start_writes(i)
-
-        attend_group(True, g, pos, k, v, lambda: k_read(g).wait(), wait_v, qa, qb, ma, mb, knew, vnew)
+        k, v = kbuf.at[g - FIRST], vbuf.at[g - FIRST]
+        attend_group(True, g, pos, k, v, lambda: k_read(g).wait(), lambda: v_read(g).wait(), qa, qb, ma, mb, knew, vnew)
+        for copy in writes(g, k, v):
+            copy.start(priority=1)
         return carry
 
-    lax.fori_loop(1, groups, step, 0)
-    start_writes(groups - 1)
+    lax.fori_loop(FIRST, groups, step, 0)
     project_out(ma, mb, wo, o_ref)
-    for copy in writes(0, kfirst, vfirst):
-        copy.wait()
-    for g in range(1, groups):
-        for copy in writes(g, kbuf.at[g - 1], vbuf.at[g - 1]):
+    for g in range(groups):
+        k, v = (kfirst[g], vfirst[g]) if g < FIRST else (kbuf.at[g - FIRST], vbuf.at[g - FIRST])
+        for copy in writes(g, k, v):
             copy.wait()
 
 
 def mlp_kernel(layer, *refs):
-    n_in, n_out = (12, 8) if layer == 0 else (6, 1)
+    n_in, n_out = (12, 6 + 2 * FIRST) if layer == 0 else (6, 1)
     x_ref, o_ref, gain_hbm, wg_hbm, wu_hbm, wd_hbm = refs[:6]
     outs = refs[n_in:n_in + n_out]
-    (x, gain, wg, wu, wd, h, ohalf, orecv1, orecv2, osum, fsend, fhalf, frecv1, frecv2, total,
-     small_sem, g_sem, u_sem, d_sem, ahead_sem, o_send, o_recv, fs1, fr1, fs2, fr2) = refs[n_in + n_out:]
+    (x, gain, wg, wu, wd, a48, h, x_other, opart, ohalf, ox, oy, oz, osum, fpart, fpair, fhalf, fx, fy, fz, fsum,
+     small_sem, w_sem, ahead_sem, o_send, o_recv, x_send, x_recv, f_send, f_recv) = refs[n_in + n_out:]
     out_ref = outs[0]
-    last = len(DOWN)
-    me = lax.axis_index("tp")
+    dp, me = lax.axis_index("dp"), lax.axis_index("tp")
     chip, core = me // 2, lax.rem(me, 2)
-    partner = chip * 2 + (1 - core)
-    across = (1 - chip) * 2 + (1 - core)
     side = lax.rem(chip + core, 2)
-
+    partner = {"dp": dp, "tp": chip * 2 + (1 - core)}
+    along = {"dp": dp, "tp": (1 - chip) * 2 + (1 - core)}
+    beside = {"dp": 1 - dp, "tp": chip * 2 + core}
+    opposite = {"dp": 1 - dp, "tp": (1 - chip) * 2 + (1 - core)}
+
+    part = pl.ds(pl.multiple_of(dp * FF_PART, FF_PART), FF_PART)
+    weights = [pltpu.make_async_copy(s, d, w_sem.at[i]) for i, (s, d) in enumerate(
+        ((wg_hbm.at[layer, :, part], wg), (wu_hbm.at[layer, :, part], wu), (wd_hbm.at[layer, part, :], wd)))]
     gain_copy = pltpu.make_async_copy(gain_hbm, gain, small_sem)
-    wide_cols = [pl.ds(start, size) for start, size in WIDE]
-    down_cols = [pl.ds(start, size) for start, size in DOWN]
-    gates = [pltpu.make_async_copy(wg_hbm.at[layer, :, d], wg.at[:, d], g_sem.at[i]) for i, d in enumerate(wide_cols)]
-    ups = [pltpu.make_async_copy(wu_hbm.at[layer, :, d], wu.at[:, d], u_sem.at[i]) for i, d in enumerate(wide_cols)]
-    downs = [pltpu.make_async_copy(wd_hbm.at[layer, :, d], wd.at[:, d], d_sem.at[i]) for i, d in enumerate(down_cols)]
     ahead = []
     if layer == 0:
         wq_hbm, wk_hbm, wv_hbm, wo_hbm, kc_hbm, vc_hbm = refs[6:12]
-        sources = [w.at[1] for w in (wq_hbm, wk_hbm, wv_hbm, wo_hbm)] + [group_rows(kc_hbm, 0), group_rows(vc_hbm, 0)]
-        ahead = [pltpu.make_async_copy(s, d, ahead_sem.at[i]) for i, (s, d) in enumerate(zip(sources, outs[2:]))]
-
-    def start_bulk(copies):
-        for copy in copies:
-            copy.start(priority=1)
+        pairs = list(zip([w.at[1] for w in (wq_hbm, wk_hbm, wv_hbm, wo_hbm)], outs[2:6]))
+        for g in range(FIRST):
+            pairs += [(group_rows(kc_hbm, g), outs[6 + g]), (group_rows(vc_hbm, g), outs[6 + FIRST + g])]
+        ahead = [pltpu.make_async_copy(s, d, ahead_sem.at[i]) for i, (s, d) in enumerate(pairs)]
 
     gain_copy.start()
-    start_bulk((gates[0], ups[0]))
+    for copy in weights:
+        copy.start(priority=1)
 
     barrier = pltpu.get_barrier_semaphore()
-    for peer in (partner, across):
-        pl.semaphore_signal(barrier, inc=1, device_id={"tp": peer}, device_id_type=pl.DeviceIdType.MESH)
-    pl.semaphore_wait(barrier, 2)
+    for peer in (partner, along, beside, opposite):
+        pl.semaphore_signal(barrier, inc=1, device_id=peer, device_id_type=pl.DeviceIdType.MESH)
+    pl.semaphore_wait(barrier, 4)
 
     def remote(src, dst, send, recv, peer):
         return pltpu.make_async_remote_copy(src_ref=src, dst_ref=dst, send_sem=send, recv_sem=recv,
-                                            device_id={"tp": peer}, device_id_type=pl.DeviceIdType.MESH)
-
-    o_copies = (remote(o_ref.at[1 - side], orecv1, o_send.at[0], o_recv.at[0], partner),
-                remote(ohalf, orecv2, o_send.at[1], o_recv.at[1], across),
-                remote(osum.at[side], osum.at[side], o_send.at[2], o_recv.at[2], partner))
+                                            device_id=peer, device_id_type=pl.DeviceIdType.MESH)
+
+    mine = pl.ds(pl.multiple_of(side * SIDE, SIDE), SIDE)
+    theirs = pl.ds(pl.multiple_of((1 - side) * SIDE, SIDE), SIDE)
+
+    o_copies = [remote(src, dst, o_send.at[i], o_recv.at[i], peer) for i, (src, dst, peer) in enumerate((
+        (o_ref.at[1 - side], opart, partner), (ohalf, oz, opposite), (ohalf, oy, beside), (ohalf, ox, along),
+        (osum.at[side], osum.at[side], partner)))]
+    x_copies = [remote(src, dst, x_send.at[i], x_recv.at[i], peer) for i, (src, dst, peer) in enumerate((
+        (x_ref.at[:, mine], x_other.at[:, mine], beside), (x_other.at[:, mine], x_other.at[:, mine], partner)))]
     o_copies[0].start()
-    start_bulk((gates[1], ups[1]))
+    x_copies[0].start()
+    for copy in ahead:
+        copy.start(priority=1)
     gain_copy.wait()
     o_copies[0].wait_recv()
-    ohalf[...] = (o_ref[side].astype(F32) + orecv1[...].astype(F32)).astype(BF16)
-    o_copies[1].start()
-    o_copies[1].wait_recv()
-    osum[side] = (ohalf[...].astype(F32) + orecv2[...].astype(F32)).astype(BF16)
-    o_copies[2].start()
-    o_copies[2].wait_recv()
-    o_sum = jnp.concatenate([osum[0], osum[1]], axis=1).astype(F32)
-    x1 = (x_ref[...].astype(F32) + normed(o_sum, gain[layer, 1:2, :]).astype(F32)).astype(BF16)
-    x[...] = x1
-    a = normed(x1.astype(F32), gain[layer, 2:3, :])
-
-    for w, (start, size) in enumerate(WIDE):
-        gates[w].wait()
-        ups[w].wait()
-        start_bulk(downs if w == 0 else ahead)
-        for c in range(start, start + size, CHUNK):
-            gate = jnp.dot(a, wg[:, c:c + CHUNK], preferred_element_type=F32)
-            up = jnp.dot(a, wu[:, c:c + CHUNK], preferred_element_type=F32)
-            h[:, c:c + CHUNK] = (jax.nn.gelu(gate, approximate=True) * up).astype(BF16)
+    ohalf[...] = (o_ref[side].astype(F32) + opart[...].astype(F32)).astype(BF16)
+    for copy in o_copies[1:4]:
+        copy.start()
+    x_copies[0].wait_recv()
+    x_copies[1].start()
+    for copy in o_copies[1:4]:
+        copy.wait_recv()
+    osum[side, 0] = (ohalf[...].astype(F32) + ox[...].astype(F32)).astype(BF16)
+    osum[side, 1] = (oy[...].astype(F32) + oz[...].astype(F32)).astype(BF16)
+    o_copies[4].start()
+    x_copies[1].wait_recv()
+    o_copies[4].wait_recv()
+    for group, rows in enumerate((x_ref, x_other)):
+        o_rows = jnp.concatenate([osum[0, group], osum[1, group]], axis=1).astype(F32)
+        x1 = (rows[...].astype(F32) + normed(o_rows, gain[layer, 1:2, :]).astype(F32)).astype(BF16)
+        if group == 0:
+            x[...] = x1
+        a48[group * ROWS:(group + 1) * ROWS, :] = normed(x1.astype(F32), gain[layer, 2:3, :])
+    weights[0].wait()
+    weights[1].wait()
+    a = a48[...]
+    for c in range(0, FF_PART, PIECE):
+        gate = jnp.dot(a, wg[:, c:c + PIECE], preferred_element_type=F32)
+        up = jnp.dot(a, wu[:, c:c + PIECE], preferred_element_type=F32)
+        h[:, c:c + PIECE] = (jax.nn.gelu(gate, approximate=True) * up).astype(BF16)
+    weights[2].wait()
     act = h[...]
 
-    def to_partner(c):
-        d = down_cols[c]
-        return remote(fsend.at[:, d], frecv1.at[:, d], fs1.at[c], fr1.at[c], partner)
-
-    def to_across(c):
-        d = down_cols[c]
-        return remote(fhalf.at[:, d], frecv2.at[:, d], fs2.at[c], fr2.at[c], across)
-
-    def relay(c):
-        d = down_cols[c]
-        to_partner(c).wait_recv()
-        fhalf[:, d] = (fsend[:, d].astype(F32) + frecv1[:, d].astype(F32)).astype(BF16)
-        to_across(c).start()
-
-    for c in range(last):
-        downs[c].wait()
-        fsend[:, down_cols[c]] = jnp.dot(act, wd[:, down_cols[c]], preferred_element_type=F32).astype(BF16)
-        to_partner(c).start()
-        if c >= 1:
-            relay(c - 1)
-    for c in range(last - 1, last):
-        relay(c)
-    squares = jnp.zeros((ROWS, HALF), F32)
-    for c in range(last):
-        to_across(c).wait_recv()
-        piece = fhalf[:, down_cols[c]].astype(F32) + frecv2[:, down_cols[c]].astype(F32)
-        total[:, down_cols[c]] = piece
-        for i in range(DOWN[c][1] // HALF):
-            lane_block = piece[:, i * HALF:(i + 1) * HALF]
-            squares = squares + lane_block * lane_block
-    inv_rms = lax.rsqrt(jnp.sum(squares, axis=-1, keepdims=True) / D + NORM_EPS)
-    branch = (total[...] * inv_rms * (1.0 + gain[layer, 3:4, :])).astype(BF16)
-    x2 = (x[...].astype(F32) + branch.astype(F32)).astype(BF16)
+    f_copies = [remote(src, dst, f_send.at[i], f_recv.at[i], peer) for i, (src, dst, peer) in enumerate((
+        (fpart.at[1 - side], fpair, partner), (fhalf.at[1], fz, opposite), (fhalf.at[1], fy, beside), (fhalf.at[0], fx, along),
+        (fsum.at[side], fsum.at[side], partner)))]
+    for which, columns in ((1 - side, theirs), (side, mine)):
+        partial = jnp.dot(act, wd[:, columns], preferred_element_type=F32)
+        fpart[which, 0] = partial[:ROWS].astype(BF16)
+        fpart[which, 1] = partial[ROWS:].astype(BF16)
+        if which is not side:
+            f_copies[0].start()
+    f_copies[0].wait_recv()
+    for group in (1, 0):
+        fhalf[group] = (fpart[side, group].astype(F32) + fpair[group].astype(F32)).astype(BF16)
+    for copy in f_copies[1:4]:
+        copy.start()
+    for copy in f_copies[1:4]:
+        copy.wait_recv()
+    fsum[side] = ((fhalf[0].astype(F32) + fx[...].astype(F32)) + (fy[...].astype(F32) + fz[...].astype(F32))).astype(BF16)
+    f_copies[4].start()
+    f_copies[4].wait_recv()
+    f_rows = jnp.concatenate([fsum[0], fsum[1]], axis=1).astype(F32)
+    x2 = (x[...].astype(F32) + normed(f_rows, gain[layer, 3:4, :]).astype(F32)).astype(BF16)
     out_ref[...] = x2
     if layer == 0:
         outs[1][...] = normed(x2.astype(F32), gain[1, 0:1, :])
-    for copy in o_copies:
+    for copy in o_copies + x_copies + f_copies:
         copy.wait_send()
-    for c in range(last):
-        to_partner(c).wait_send()
-        to_across(c).wait_send()
     for copy in ahead:
         copy.wait()
 
@@ -378,25 +367,25 @@
 
 def global_call(pos, a, cos_part, sin_part, ahead, kc, vc):
     groups, n = ROWS // GROUP, kc.shape[1]
-    first = pltpu.VMEM((GROUP, n, HEAD), BF16)
+    first = (pltpu.VMEM((GROUP, n, HEAD), BF16),) * (2 * FIRST)
+    rest = groups - FIRST
     return pl.pallas_call(
         global_kernel,
         name="global_attention",
         out_shape=(jax.ShapeDtypeStruct(kc.shape, BF16), jax.ShapeDtypeStruct(vc.shape, BF16),
-                   pltpu.VMEM((2, ROWS, SIDE), BF16), first, first),
-        in_specs=[ANY] + [IN_VMEM] * 9 + [ANY] * 2,
-        out_specs=(IN_HBM, IN_HBM, IN_VMEM, IN_VMEM, IN_VMEM),
-        input_output_aliases={8: 3, 9: 4},
+                   pltpu.VMEM((2, ROWS, SIDE), BF16)) + first,
+        in_specs=[ANY] + [IN_VMEM] * (7 + 2 * FIRST) + [ANY] * 2,
+        out_specs=(IN_HBM, IN_HBM) + (IN_VMEM,) * (1 + 2 * FIRST),
+        input_output_aliases={8 + i: 3 + i for i in range(2 * FIRST)},
         scratch_shapes=[
             pltpu.SMEM((ROWS,), jnp.int32),
-            pltpu.VMEM((groups - 1, GROUP, n, HEAD), BF16), pltpu.VMEM((groups - 1, GROUP, n, HEAD), BF16),
-        ] + head_scratch() + [DMA(())] + [DMA((groups - 1,))] * 2 + [DMA((groups,))] * 2,
-        compiler_params=pltpu.CompilerParams(vmem_limit_bytes=42 * MIB),
+            pltpu.VMEM((rest, GROUP, n, HEAD), BF16), pltpu.VMEM((rest, GROUP, n, HEAD), BF16),
+        ] + head_scratch() + [DMA(())] + [DMA((rest,))] * 2 + [DMA((groups,))] * 2,
+        compiler_params=pltpu.CompilerParams(vmem_limit_bytes=27 * MIB),
     )(in_hbm(pos), *[in_vmem(v) for v in (a, cos_part, sin_part, *ahead)], in_hbm(kc), in_hbm(vc))
 
 
 def mlp_call(layer, x, o, gains, wg, wu, wd, ahead=()):
-    square = pltpu.VMEM((D, D), BF16)
     full = pltpu.VMEM((ROWS, D), BF16)
     side = pltpu.VMEM((ROWS, SIDE), BF16)
     both = pltpu.VMEM((2, ROWS, SIDE), BF16)
@@ -404,7 +393,7 @@
     out_shape = [rows]
     if ahead:
         out_shape += [rows] + [pltpu.VMEM(w.shape[1:], BF16) for w in ahead[:4]]
-        out_shape += [pltpu.VMEM((GROUP,) + c.shape[1:], BF16) for c in ahead[4:]]
+        out_shape += [pltpu.VMEM((GROUP,) + c.shape[1:], BF16) for c in ahead[4:] for _ in range(FIRST)]
     return pl.pallas_call(
         functools.partial(mlp_kernel, layer),
         name=f"mlp{layer}",
@@ -412,11 +401,13 @@
         in_specs=[IN_VMEM] * 2 + [ANY] * (4 + len(ahead)),
         out_specs=[IN_VMEM] * len(out_shape),
         scratch_shapes=[
-            full, pltpu.VMEM((2, 4, D), F32), square, square, square, full,
-            side, side, side, both, full, full, full, full, pltpu.VMEM((ROWS, D), F32),
-            DMA(()), DMA((len(WIDE),)), DMA((len(WIDE),)), DMA((len(DOWN),)), DMA((6,)), DMA((3,)), DMA((3,)),
-        ] + [DMA((len(DOWN),))] * 4,
-        compiler_params=pltpu.CompilerParams(collective_id=layer, has_side_effects=True, vmem_limit_bytes=40 * MIB),
+            full, pltpu.VMEM((2, 4, D), F32), pltpu.VMEM((D, FF_PART), BF16), pltpu.VMEM((D, FF_PART), BF16), pltpu.VMEM((FF_PART, D), BF16),
+            pltpu.VMEM((2 * ROWS, D), BF16), pltpu.VMEM((2 * ROWS, FF_PART), BF16),
+            full, side, side, side, side, side, pltpu.VMEM((2, 2, ROWS, SIDE), BF16),
+            pltpu.VMEM((2, 2, ROWS, SIDE), BF16), both, both, side, side, side, both,
+            DMA(()), DMA((3,)), DMA((4 + 2 * FIRST,)), DMA((5,)), DMA((5,)), DMA((2,)), DMA((2,)), DMA((5,)), DMA((5,)),
+        ],
+        compiler_params=pltpu.CompilerParams(collective_id=layer, has_side_effects=True, vmem_limit_bytes=24 * MIB),
     )(in_vmem(x), in_vmem(o), *[in_hbm(v) for v in (gains, wg, wu, wd) + tuple(ahead)])
 
 
@@ -429,7 +420,7 @@
     kg, vg = flat(k_global), flat(v_global)
     kl_new, vl_new, o, cos_part, sin_part, x = local_call(positions, hidden, norm_scale, freq, w_query, w_key, w_value, w_out, flat(k_local), flat(v_local))
     x, a, *ahead = mlp_call(0, x, o, norm_scale, w_gate, w_up, w_down, (w_query, w_key, w_value, w_out, kg, vg))
-    kg_new, vg_new, o, _, _ = global_call(positions, a, cos_part, sin_part, ahead, kg, vg)
+    kg_new, vg_new, o, *_ = global_call(positions, a, cos_part, sin_part, ahead, kg, vg)
     (x,) = mlp_call(1, x, o, norm_scale, w_gate, w_up, w_down)
     return (x, kl_new.reshape(k_local.shape), vl_new.reshape(v_local.shape), kg_new.reshape(k_global.shape), vg_new.reshape(v_global.shape))
 

time: 86.9 us -> 83.8 us (0.964)
  Pallas kernels: 85.5 us -> 82.3 us
    pallas_call x1, Pallas kernels: 30.2 us -> 23.9 us  [global_call(): pl.pallas_call(global_kernel, name='global_attention', out_shape=(jax.Sha...]
    pallas_call x2, Pallas kernels: 37.6 us -> 40.8 us  [mlp_call(): pl.pallas_call(functools.partial(mlp_kernel, layer), name=f'mlp{layer}',...]
where the time goes in v5:
time: 83.8 us; the launch traced here: 83.7 us
  Pallas kernels  82.3 us (98%)
    pallas_call x2, Pallas kernels, mlp_call(): pl.pallas_call(functools.partial(mlp_kernel, layer), name=f'mlp{layer}',...  40.8 us
    pallas_call x1, Pallas kernels, global_call(): pl.pallas_call(global_kernel, name='global_attention', out_shape=(jax.Sha...  23.9 us
    pallas_call x1, Pallas kernels, local_call(): pl.pallas_call(local_kernel, name='local_attention', out_shape=(jax.Shape...  17.7 us

profile of v5, /device:TPU:0, one launch (start us, length us, event | category | flops | bytes accessed | tf_op | source)
XLA Modules:
  0.0 83.7 jit_solution(8664827798111981738)
XLA Ops:
  0.6 17.7 %local_attention.1 = (bf16[24,1024,256]{2,1,0:T(8,128)(2,1)}, bf16[24,1024,256]{2,1,0:T(8,128)(2,1)}, bf16[2,24,1280]{2,1,0:T(8,128)(2,1)S(1)}, f32[24,128]{1,0:...) custom-call(s32[24]{0:T(128)} %pos_hbm.3, bf16[24,2560]{1,0:T(8,128)(2,1)} %x_hbm.1, ...), custom_call_target="tpu_custom_call" | custom-call | tf_op jit(solution)/shard_map/local_attention/pallas_call | solution.py:351
  18.4 22.0 %mlp0.1 = (bf16[24,2560]{1,0:T(8,128)(2,1)S(1)}, bf16[24,2560]{1,0:T(8,128)(2,1)S(1)}, bf16[2560,512]{1,0:T(8,128)(2,1)S(1)}, bf16[2560,256]{1,0:T(8,128)(2,1)S(...) custom-call(bf16[24,2560]{1,0:T(8,128)(2,1)S(1)} %get-tuple-element., ...), custom_call_target="tpu_custom_call" | custom-call | tf_op jit(solution)/shard_map/mlp0/pallas_call | solution.py:397
  40.4 23.9 %global_attention.1 = (bf16[24,2048,256]{2,1,0:T(8,128)(2,1)}, bf16[24,2048,256]{2,1,0:T(8,128)(2,1)}, bf16[2,24,1280]{2,1,0:T(8,128)(2,1)S(1)}, bf16[4,2048,256...) custom-call(s32[24]{0:T(128)} %pos_hbm.3, ...), custom_call_target="tpu_custom_call", output_to_operand_aliasing={{3}: (8, {}), {4}: (9, {}), {5}: (10, {}), {6}: (11, {}), {... | custom-call | tf_op jit(solution)/shard_map/global_attention/pallas_call | solution.py:372
  64.2 18.8 %mlp1.1 = bf16[24,2560]{1,0:T(8,128)(2,1)S(1)} custom-call(bf16[24,2560]{1,0:T(8,128)(2,1)S(1)} %get-tuple-element.28.refs_0_, bf16[2,24,1280]{2,1,0:T(8,128)(2,1)S(1)} %get-tuple-element.42.refs_1_, f32[2,4,2560]{2,1,0:T(4,128)} %refs_2_.3, bf16[2,2560,2560]{2,1,0:T(8,128)(2,1)} %refs_3_.3, bf16[2,2560,2560]{2,1,0:T(8,128)(2,1)} %refs_4_.3, ...), custom_call_target="tpu_custom_call" | custom-call | tf_op jit(solution)/shard_map/mlp1/pallas_call | solution.py:397
  83.0 0.7 copy.37

commit v6 on v5

--- a/solution.py
+++ b/solution.py
@@ -22,6 +22,7 @@
 FIRST = 3
 FF_PART = D // 2
 PIECE = 256
+PARTS = ((0, 512), (512, 768))
 F32 = jnp.float32
 BF16 = jnp.bfloat16
 
@@ -297,31 +298,48 @@
     weights[2].wait()
     act = h[...]
 
-    f_copies = [remote(src, dst, f_send.at[i], f_recv.at[i], peer) for i, (src, dst, peer) in enumerate((
-        (fpart.at[1 - side], fpair, partner), (fhalf.at[1], fz, opposite), (fhalf.at[1], fy, beside), (fhalf.at[0], fx, along),
-        (fsum.at[side], fsum.at[side], partner)))]
-    for which, columns in ((1 - side, theirs), (side, mine)):
+    def f_exchange(j):
+        cut = pl.ds(*PARTS[j])
+        return [remote(src, dst, f_send.at[j, i], f_recv.at[j, i], peer) for i, (src, dst, peer) in enumerate((
+            (fpart.at[1 - side, :, :, cut], fpair.at[:, :, cut], partner), (fhalf.at[1, :, cut], fz.at[:, cut], opposite),
+            (fhalf.at[1, :, cut], fy.at[:, cut], beside), (fhalf.at[0, :, cut], fx.at[:, cut], along),
+            (fsum.at[side, :, cut], fsum.at[side, :, cut], partner)))]
+
+    f_copies = [f_exchange(j) for j in range(len(PARTS))]
+
+    def down(which, j):
+        start, size = PARTS[j]
+        columns = pl.ds(pl.multiple_of(which * SIDE + start, PIECE), size)
         partial = jnp.dot(act, wd[:, columns], preferred_element_type=F32)
-        fpart[which, 0] = partial[:ROWS].astype(BF16)
-        fpart[which, 1] = partial[ROWS:].astype(BF16)
-        if which is not side:
-            f_copies[0].start()
-    f_copies[0].wait_recv()
-    for group in (1, 0):
-        fhalf[group] = (fpart[side, group].astype(F32) + fpair[group].astype(F32)).astype(BF16)
-    for copy in f_copies[1:4]:
-        copy.start()
-    for copy in f_copies[1:4]:
-        copy.wait_recv()
-    fsum[side] = ((fhalf[0].astype(F32) + fx[...].astype(F32)) + (fy[...].astype(F32) + fz[...].astype(F32))).astype(BF16)
-    f_copies[4].start()
-    f_copies[4].wait_recv()
+        for group in range(2):
+            fpart[which, group, :, start:start + size] = partial[group * ROWS:(group + 1) * ROWS].astype(BF16)
+
+    for j, copies in enumerate(f_copies):
+        down(1 - side, j)
+        copies[0].start()
+    for j, copies in enumerate(f_copies):
+        cut = pl.ds(*PARTS[j])
+        down(side, j)
+        copies[0].wait_recv()
+        for group in (1, 0):
+            fhalf[group, :, cut] = (fpart[side, group, :, cut].astype(F32) + fpair[group, :, cut].astype(F32)).astype(BF16)
+        for copy in copies[1:4]:
+            copy.start()
+    for j, copies in enumerate(f_copies):
+        cut = pl.ds(*PARTS[j])
+        for copy in copies[1:4]:
+            copy.wait_recv()
+        near = fhalf[0, :, cut].astype(F32) + fx[:, cut].astype(F32)
+        fsum[side, :, cut] = (near + (fy[:, cut].astype(F32) + fz[:, cut].astype(F32))).astype(BF16)
+        copies[4].start()
+    for copies in f_copies:
+        copies[4].wait_recv()
     f_rows = jnp.concatenate([fsum[0], fsum[1]], axis=1).astype(F32)
     x2 = (x[...].astype(F32) + normed(f_rows, gain[layer, 3:4, :]).astype(F32)).astype(BF16)
     out_ref[...] = x2
     if layer == 0:
         outs[1][...] = normed(x2.astype(F32), gain[1, 0:1, :])
-    for copy in o_copies + x_copies + f_copies:
+    for copy in o_copies + x_copies + f_copies[0] + f_copies[1]:
         copy.wait_send()
     for copy in ahead:
         copy.wait()
@@ -405,7 +423,7 @@
             pltpu.VMEM((2 * ROWS, D), BF16), pltpu.VMEM((2 * ROWS, FF_PART), BF16),
             full, side, side, side, side, side, pltpu.VMEM((2, 2, ROWS, SIDE), BF16),
             pltpu.VMEM((2, 2, ROWS, SIDE), BF16), both, both, side, side, side, both,
-            DMA(()), DMA((3,)), DMA((4 + 2 * FIRST,)), DMA((5,)), DMA((5,)), DMA((2,)), DMA((2,)), DMA((5,)), DMA((5,)),
+            DMA(()), DMA((3,)), DMA((4 + 2 * FIRST,)), DMA((5,)), DMA((5,)), DMA((2,)), DMA((2,)), DMA((2, 5)), DMA((2, 5)),
         ],
         compiler_params=pltpu.CompilerParams(collective_id=layer, has_side_effects=True, vmem_limit_bytes=24 * MIB),
     )(in_vmem(x), in_vmem(o), *[in_hbm(v) for v in (gains, wg, wu, wd) + tuple(ahead)])

time: 83.8 us -> 83.1 us (level)
  no operation moved by 1% of the time
where the time goes in v6:
time: 83.1 us
  Pallas kernels  81.7 us (98%)
    pallas_call x2, Pallas kernels, mlp_call(): pl.pallas_call(functools.partial(mlp_kernel, layer), name=f'mlp{layer}',...  40.2 us
    pallas_call x1, Pallas kernels, global_call(): pl.pallas_call(global_kernel, name='global_attention', out_shape=(jax.Sha...  23.9 us
    pallas_call x1, Pallas kernels, local_call(): pl.pallas_call(local_kernel, name='local_attention', out_shape=(jax.Shape...  17.7 us

profile of v6, /device:TPU:0, one launch (start us, length us, event | category | flops | bytes accessed | tf_op | source)
XLA Modules:
  0.0 83.1 jit_solution(13808613970305731409)
XLA Ops:
  0.6 17.7 %local_attention.1 = (bf16[24,1024,256]{2,1,0:T(8,128)(2,1)}, bf16[24,1024,256]{2,1,0:T(8,128)(2,1)}, bf16[2,24,1280]{2,1,0:T(8,128)(2,1)S(1)}, f32[24,128]{1,0:...) custom-call(s32[24]{0:T(128)} %pos_hbm.3, bf16[24,2560]{1,0:T(8,128)(2,1)} %x_hbm.1, ...), custom_call_target="tpu_custom_call" | custom-call | tf_op jit(solution)/shard_map/local_attention/pallas_call | solution.py:369
  18.4 21.4 %mlp0.1 = (bf16[24,2560]{1,0:T(8,128)(2,1)S(1)}, bf16[24,2560]{1,0:T(8,128)(2,1)S(1)}, bf16[2560,512]{1,0:T(8,128)(2,1)S(1)}, bf16[2560,256]{1,0:T(8,128)(2,1)S(...) custom-call(bf16[24,2560]{1,0:T(8,128)(2,1)S(1)} %get-tuple-element., ...), custom_call_target="tpu_custom_call" | custom-call | tf_op jit(solution)/shard_map/mlp0/pallas_call | solution.py:415
  39.7 23.9 %global_attention.1 = (bf16[24,2048,256]{2,1,0:T(8,128)(2,1)}, bf16[24,2048,256]{2,1,0:T(8,128)(2,1)}, bf16[2,24,1280]{2,1,0:T(8,128)(2,1)S(1)}, bf16[4,2048,256...) custom-call(s32[24]{0:T(128)} %pos_hbm.3, ...), custom_call_target="tpu_custom_call", output_to_operand_aliasing={{3}: (8, {}), {4}: (9, {}), {5}: (10, {}), {6}: (11, {}), {... | custom-call | tf_op jit(solution)/shard_map/global_attention/pallas_call | solution.py:390
  63.6 18.8 %mlp1.1 = bf16[24,2560]{1,0:T(8,128)(2,1)S(1)} custom-call(bf16[24,2560]{1,0:T(8,128)(2,1)S(1)} %get-tuple-element.28.refs_0_, bf16[2,24,1280]{2,1,0:T(8,128)(2,1)S(1)} %get-tuple-element.42.refs_1_, f32[2,4,2560]{2,1,0:T(4,128)} %refs_2_.3, bf16[2,2560,2560]{2,1,0:T(8,128)(2,1)} %refs_3_.3, bf16[2,2560,2560]{2,1,0:T(8,128)(2,1)} %refs_4_.3, ...), custom_call_target="tpu_custom_call" | custom-call | tf_op jit(solution)/shard_map/mlp1/pallas_call | solution.py:415
  82.4 0.7 copy.37
